TPU v7x, 32 devices: a whole 2x2x4 slice. The times are simulated.
32 devices in a mesh: dp: 8 (over y, x, core), seq: 4 (over z).
Axes of the slice: x: 2, y: 2, z: 4, core: 2. Of those that a mesh axis runs over, the one named last changes fastest.
Arguments:
- inputs: float32 [16, 768, 512], P('dp', 'seq'), may hold values from -6 to 6
- lengths: int32 [16], P('dp'), may hold values from 192 to 768, as said below
- rel_bucket: int32 [1535], replicated, may hold values from 0 to 31
- params: float32 [6059776], P(('dp', 'seq')), may hold values from -3 to 3, as said below
- moment_one: float32 [6059776], P(('dp', 'seq')), may hold values from -12288 to 12288
- moment_two: float32 [6059776], P(('dp', 'seq')), may hold values from 0 to 12288, as said below
- cotangent: float32 [16, 768, 512], P('dp', 'seq'), may hold values from -6 to 6
Outputs:
- block_output: float32 [16, 768, 512], P('dp', 'seq')
- input_grad: float32 [16, 768, 512], P('dp', 'seq')
- param_grad: float32 [6059776], P(('dp', 'seq'))
- new_params: float32 [6059776], P(('dp', 'seq'))
- new_moment_one: float32 [6059776], P(('dp', 'seq'))
- new_moment_two: float32 [6059776], P(('dp', 'seq'))
Inputs may be any that keep to these rules, and one draw needn't show every extreme that they name: `lengths`: some sequence is 768 tokens long in every draw. `params`: norm and batch-norm gains lie in 0.5 to 1.5. `moment_two`: every entry is positive.
All inputs are finite; a program needn't handle non-finite values.
Results may differ from a plain program's by a relative error of at most 0.012.
Values may be sent and summed in bfloat16 or wider, within the bound.
A program may use at most 256 MiB of HBM per device.

v0:
```python
import functools
import math

import jax
import jax.numpy as jnp
from jax import lax
from jax.experimental import pallas as pl
from jax.experimental.pallas import tpu as pltpu
from jax.sharding import PartitionSpec as P

D = 512
H = 8
HD = 64
FF = 2048
K = 31
NB = 32
DP = "dp"
SEQ = "seq"
STEP = 4


NORM_EPS = 1e-05
BATCH_EPS = 1e-05
LEARN_RATE = 0.005
DECAY = 0.01
BETA_ONE = 0.9
BETA_TWO = 0.98
ADAM_EPS = 1e-08


def segments():

    def feed_block(prefix):
        return [
            (prefix + "_ng", (D,)),
            (prefix + "_nb", (D,)),
            (prefix + "_w_in", (D, FF)),
            (prefix + "_b_in", (FF,)),
            (prefix + "_w_out", (FF, D)),
            (prefix + "_b_out", (D,)),
        ]

    listing = feed_block("first")
    listing = listing + [
        ("attn_ng", (D,)),
        ("attn_nb", (D,)),
        ("w_q", (D, D)),
        ("b_q", (D,)),
        ("w_k", (D, D)),
        ("w_v", (D, D)),
        ("b_v", (D,)),
        ("w_o", (D, D)),
        ("b_o", (D,)),
        ("rel", (NB, H)),
    ]
    listing = listing + [
        ("conv_ng", (D,)),
        ("conv_nb", (D,)),
        ("w_pi", (D, 2 * D)),
        ("b_pi", (2 * D,)),
        ("w_depth", (K, D)),
        ("bng", (D,)),
        ("bnb", (D,)),
        ("w_po", (D, D)),
        ("b_po", (D,)),
    ]
    listing = listing + feed_block("second") + [("fin_g", (D,)), ("fin_b", (D,))]
    return listing


def arrange():
    places, gaps = {}, []
    linear = inner = 0
    for entry_name, entry_shape in segments():
        extent = math.prod(entry_shape)
        tail = 2 * D if entry_name == "conv_ng" else 0
        if extent >= D * D or tail:
            pad = -(inner + tail) % TILE
            if pad:
                gaps.append((linear, pad))
                inner = inner + pad
        places[entry_name] = inner // LANES
        linear, inner = linear + extent, inner + extent
    return places, gaps, -(-inner // TILE)


def device_index():
    return lax.axis_index(DP) * lax.axis_size(SEQ) + lax.axis_index(SEQ)


def own_shard(plan, window):
    table = jnp.asarray(plan.shard_table, jnp.int32)[device_index()]
    flat = window.reshape(-1)
    early = lax.dynamic_slice(flat, (table[0],), (plan.shard,))
    late = lax.dynamic_slice(flat, (table[0] + table[2],), (plan.shard,))
    return jnp.where(jnp.arange(plan.shard, dtype=jnp.int32) < table[1], early, late)


def swish_act(values):
    return values * jax.nn.sigmoid(values)


def swish_grad(values):
    sig_vals = jax.nn.sigmoid(values)
    return sig_vals * (1.0 + values * (1.0 - sig_vals))


def forward_dot(left_mat, weight):
    return jnp.dot(left_mat, weight, preferred_element_type=jnp.float32)


def back_dot(grad_in, weight):
    return lax.dot_general(
        grad_in, weight, (((1,), (1,)), ((), ())), preferred_element_type=jnp.float32
    )


MESH = pl.DeviceIdType.MESH
LANES=512
TILE=8*LANES

class Plan:
    def __init__(self, ndp, nseq, shard):
        self.ndp, self.nseq, self.shard = ndp, nseq, shard
        self.k = ndp.bit_length() - 1
        self.phases = self.k - 1
        self.n = n = ndp * nseq
        self.places, self.gaps, self.total = arrange()
        begins = [self.inner(d * shard) for d in range(n)]
        starts = [-(-b // TILE) for b in begins] + [self.total]
        sizes = [b - a for a, b in zip(starts, starts[1:])]
        self.lo, self.hi = min(sizes), max(sizes)
        self.slots = nseq * 2**self.phases
        floors = [b // TILE for b in begins]
        ends = [self.inner((d + 1) * shard - 1) // TILE + 1 for d in range(n)]
        self.win = max(e - f for e, f in zip(ends, floors))
        self.win += self.win % 2
        self.padded = max(self.total, max(floors) + self.win)
        self.block_table, self.shard_table = [], []
        for d in range(n):
            near = [g for g in self.gaps if d * shard < g[0] < (d + 1) * shard + TILE]
            assert len(near) <= 1
            cut, size = near[0] if near else (2**30, 0)
            lead = starts[d] * TILE - begins[d]
            self.block_table.append((lead, cut - d * shard - lead, size))
            self.shard_table.append((begins[d] - floors[d] * TILE, cut - d * shard, size))

    def inner(self, position):
        if isinstance(position, int):
            return position + sum(size for at, size in self.gaps if at <= position)
        result = position
        for at, size in self.gaps:
            result = result + jnp.where(position >= at, size, 0)
        return result

    def order(self):
        ev=[]
        for s in range(self.nseq):
            for sign in ((0,) if s==0 else (-1,1)):
                for t in range(2**self.phases):
                    ev.append((s+0.5*bin(t).count("1")+0.01*t, s, sign, t))
        ev.sort()
        return [e[1:] for e in ev]

def flip(di, mask_bits, bits, t, phases):
    out=di
    for p in range(phases):
        if (t>>p)&1:
            out = out + mask_bits[p]*(1-2*bits[p])
    return out

def phase_masks(di, c, phases):
    masks, bits=[],[]
    for p in range(phases):
        a, b = 1<<(p+1), 1<<(phases-p)
        masks.append(a+c*(b-a))
        ba, bb = (di//a)%2, (di//b)%2
        bits.append(ba+c*(bb-ba))
    return masks, bits

def block_of(plan, dpi, z):
    d = dpi*plan.nseq+z
    a = (plan.inner(d*plan.shard)+TILE-1)//TILE
    b = (plan.inner((d+1)*plan.shard)+TILE-1)//TILE
    b = jnp.where(d == plan.n-1, plan.total, b)
    return a, b-a

def floor_of(plan, dpi, z):
    return plan.inner((dpi*plan.nseq+z)*plan.shard)//TILE

FRONT, NEAR, BACK = 32, 40, 64


def shard_rows(plan):
    return -(-plan.shard // 1024) * 8


def place_rows(plan, rolled, block, first, rows, lead, cut, skip):
    shift, begin = lead % 128, FRONT + lead // 128
    lane = lax.broadcasted_iota(jnp.int32, (rows, 128), 1)
    at = (lax.broadcasted_iota(jnp.int32, (rows, 128), 0) + first) * LANES + lane
    for j in range(LANES // 128):

        def read(start):
            here = rolled[pl.ds(start, rows, stride=4), :]
            after = rolled[pl.ds(start + 1, rows, stride=4), :]
            return jnp.where(lane < 128 - shift, here, after)

        start = begin + j + 4 * first
        value = jnp.where(at + 128 * j < cut, read(start), read(start - skip)).astype(block.dtype)
        part = slice(first // 8, (first + rows) // 8)
        block[part, :, j * 128 : (j + 1) * 128] = value.reshape(rows // 8, 8, 128)


def gather_kernel(plan, x, out, src, line, rolled, give, take, near_sem, send_a, send_b, recv_a, recv_b, loc_sem):
    di, z = lax.axis_index(DP), lax.axis_index(SEQ)
    ns, ph = plan.nseq, plan.phases
    c = di%2
    masks, bits = phase_masks(di, c, ph)
    other = di+1-2*c
    omasks, obits = phase_masks(other, 1-c, ph)
    up, down = lax.rem(z+1,ns), lax.rem(z+ns-1,ns)
    partners=[(di,up),(di,down),(other,z)]+[(flip(di,masks,bits,1<<p,ph),z) for p in range(ph)]
    barrier=pltpu.get_barrier_semaphore()
    for a,b in partners:
        pl.semaphore_signal(barrier,inc=1,device_id=(a,b),device_id_type=MESH)
    index = di * ns + z
    following, before = lax.rem(index + 1, plan.n), lax.rem(index + plan.n - 1, plan.n)
    pl.semaphore_signal(barrier, inc=1, device_id=(following // ns, lax.rem(following, ns)), device_id_type=MESH)
    lo, more = plan.lo-1, plan.hi-plan.lo+1
    start_own, size_own = block_of(plan, di, z)
    rows = x.shape[0]
    joint, shift = divmod(plan.shard, 128)
    lane = lax.broadcasted_iota(jnp.int32, (NEAR, 128), 1)
    moved = pltpu.roll(x[:NEAR], shift, 1)
    earlier = jnp.concatenate([jnp.zeros((1, 128), jnp.float32), moved[: NEAR - 1]], 0)
    give[...] = jnp.where(lane >= shift, moved, earlier)
    line[:FRONT] = jnp.zeros((FRONT, 128), jnp.float32)
    line[FRONT : FRONT + rows] = x[...]
    line[FRONT + rows :] = jnp.zeros((line.shape[0] - FRONT - rows, 128), jnp.float32)
    begin = index * plan.shard
    inner = plan.inner(begin)
    lead = (inner + TILE - 1) // TILE * TILE - inner
    cut, skip = 2**30, 0
    for position, size in plan.gaps:
        hit = jnp.logical_and(position > begin, position < begin + plan.shard + TILE)
        cut = jnp.where(hit, position - begin - lead, cut)
        skip = jnp.where(hit, size // 128, skip)
    turn = lax.rem(128 - lead % 128, 128)
    rolled[...] = pltpu.roll(line[...], turn, 1)
    place_rows(plan, rolled, src, 0, 8 * lo, lead, cut, skip)
    pl.semaphore_wait(barrier,len(partners)+1)
    near = pltpu.make_async_remote_copy(src_ref=give,dst_ref=take,send_sem=near_sem.at[0],recv_sem=near_sem.at[1],
        device_id=(before // ns, lax.rem(before, ns)),device_id_type=MESH)
    near.start()

    def pair(ref, base, dst_start, size, sidx, ridx, dev):
        copies=[pltpu.make_async_remote_copy(src_ref=ref.at[pl.ds(base,lo)],dst_ref=out.at[pl.ds(dst_start,lo)],
            send_sem=send_a.at[sidx],recv_sem=recv_a.at[ridx],device_id=dev,device_id_type=MESH)]
        for x in range(more):
            copies.append(pltpu.make_async_remote_copy(src_ref=ref.at[pl.ds(base+lo+x,1)],dst_ref=out.at[pl.ds(dst_start+lo+x,1)],
                send_sem=send_b.at[sidx*more+x],recv_sem=recv_b.at[ridx*more+x],device_id=dev,device_id_type=MESH))
        return copies, size
    def each(p, act, part=None):
        for x,copy in enumerate(p[0]):
            if part is not None and (x==0) != (part==0): continue
            if x<2: act(copy)
            else:
                @pl.when(p[1]>=lo+x)
                def _(): act(copy)
    def start(p,part): each(p, lambda c: c.start(), part)
    def wait_send(p): each(p, lambda c: c.wait_send())
    def wait_recv(p,part=None): each(p, lambda c: c.wait_recv(), part)

    own=[pltpu.make_async_copy(src.at[pl.ds(0,lo)],out.at[pl.ds(start_own,lo)],loc_sem.at[0])]
    for x in range(more):
        own.append(pltpu.make_async_copy(src.at[pl.ds(lo+x,1)],out.at[pl.ds(start_own+lo+x,1)],loc_sem.at[1+x]))
    own=(own,size_own)
    own[0][0].start()
    def finish_block():
        near.wait_recv()
        at = FRONT + joint
        line[at:at+1] = line[at:at+1] + take[0:1]
        line[at+1:at+NEAR] = take[1:]
        low = at // 8 * 8
        rolled[low:] = pltpu.roll(line[low:], turn, 1)
        place_rows(plan, rolled, src, 8*lo, 8*more, lead, cut, skip)
        for x,copy in enumerate(own[0][1:]):
            if x==0: copy.start()
            else:
                @pl.when(size_own>lo+x)
                def _(): copy.start()
    nslot=plan.slots
    sends=[]
    def guard(conds, fn):
        if not conds: fn(); return
        cond=conds[0]
        for x in conds[1:]: cond=jnp.logical_and(cond,x)
        @pl.when(cond)
        def _(): fn()

    tasks=[]
    for s, sign, t in plan.order():
        zz = z+sign*s
        conds=[] if s==0 else ([zz>=0] if sign<0 else [zz<ns])
        dpi=flip(di,masks,bits,t,ph)
        st,size=block_of(plan,dpi,zz)
        mine = s==0 and t==0
        ref, base = (src, 0) if mine else (out, st)
        slot = t*ns+zz
        got = None if mine else pair(out,st,st,size,0,slot,(di,z))
        copies=[]
        def forward(conds, ridx, dev):
            p=pair(ref,base,st,size,len(sends),ridx,dev)
            sends.append((conds,p))
            copies.append((conds,p))
        if t==0:
            if sign<=0 : forward(conds+[z<ns-1],slot,(di,z+1))
            if sign>=0 : forward(conds+[z>0],slot,(di,z-1))
        for pp in range(t.bit_length(),ph):
            forward(conds,slot+(1<<pp)*ns,(flip(di,masks,bits,1<<pp,ph),z))
        forward(conds,nslot+slot,(other,z))
        tasks.append((conds,got,copies))
    def run(task,part):
        conds,got,copies=task
        if got is None:
            if part==1: finish_block()
        else:
            guard(conds, lambda: wait_recv(got,part))
        for also,p in copies:
            guard(also, lambda: start(p,part))
    lag=4
    for i in range(len(tasks)+lag):
        if i<len(tasks): run(tasks[i],0)
        if i>=lag: run(tasks[i-lag],1)
    for s, sign, t in plan.order():
        zz=z+sign*s
        conds=[] if s==0 else ([zz>=0] if sign<0 else [zz<ns])
        dpi=flip(other,omasks,obits,t,ph)
        st,size=block_of(plan,dpi,zz)
        p=pair(out,st,st,size,0,nslot+t*ns+zz,(di,z))
        guard(conds,lambda: wait_recv(p))
    for conds,p in sends:
        guard(conds,lambda: wait_send(p))
    each(own, lambda c: c.wait())
    near.wait_send()

def count_sends(plan):
    n=0
    for s,sign,t in plan.order():
        if t==0: n+= (2 if sign==0 else 1)
        n+=plan.phases-t.bit_length()+1
    return n

def gather(plan, params):
    ns, more = count_sends(plan), plan.hi - plan.lo + 1
    rows = shard_rows(plan)
    lines = FRONT + rows + NEAR + BACK
    lines += -lines % 8
    values = jnp.pad(params, (0, rows * 128 - plan.shard)).reshape(rows, 128)
    return pl.pallas_call(
        functools.partial(gather_kernel, plan),
        out_shape=jax.ShapeDtypeStruct((plan.total, 8, LANES), jnp.bfloat16),
        in_specs=[pl.BlockSpec(memory_space=pltpu.VMEM)],
        out_specs=pl.BlockSpec(memory_space=pl.ANY),
        scratch_shapes=[
            pltpu.VMEM((plan.hi, 8, LANES), jnp.bfloat16), pltpu.VMEM((lines, 128), jnp.float32),
            pltpu.VMEM((lines, 128), jnp.float32), pltpu.VMEM((NEAR, 128), jnp.float32),
            pltpu.VMEM((NEAR, 128), jnp.float32), pltpu.SemaphoreType.DMA((2,)),
            pltpu.SemaphoreType.DMA((ns,)), pltpu.SemaphoreType.DMA((ns * more,)),
            pltpu.SemaphoreType.DMA((2 * plan.slots,)), pltpu.SemaphoreType.DMA((2 * plan.slots * more,)),
            pltpu.SemaphoreType.DMA((1 + more,)),
        ],
        compiler_params=pltpu.CompilerParams(collective_id=0, has_side_effects=True),
        name="gather_params",
    )(values)


def scatter_kernel(plan, g, out, acc, rc, rp, rz, load_sem, send_sem, core_send, core_recv, ph_recv, z_recv):
    di, z = lax.axis_index(DP), lax.axis_index(SEQ)
    ns, ph, win, nslot = plan.nseq, plan.phases, plan.win, plan.slots
    c = di%2
    masks, bits = phase_masks(di, c, ph)
    other = di+1-2*c
    omasks, obits = phase_masks(other, 1-c, ph)
    up, down = lax.rem(z+1,ns), lax.rem(z+ns-1,ns)
    partners=[(di,up),(di,down),(other,z)]+[(flip(di,masks,bits,1<<p,ph),z) for p in range(ph)]
    barrier=pltpu.get_barrier_semaphore()
    for a,b in partners:
        pl.semaphore_signal(barrier,inc=1,device_id=(a,b),device_id_type=MESH)
    order=list(reversed(plan.order()))
    def cond_of(s,sign):
        zz=z+sign*s
        return zz,([] if s==0 else ([zz>=0] if sign<0 else [zz<ns]))
    def guard(conds, fn):
        if not conds: fn(); return
        cond=conds[0]
        for x in conds[1:]: cond=jnp.logical_and(cond,x)
        @pl.when(cond)
        def _(): fn()
    def load(s,sign,t):
        zz,conds=cond_of(s,sign)
        slot=t*ns+zz
        st=floor_of(plan,flip(di,masks,bits,t,ph),zz)
        return conds,pltpu.make_async_copy(g.at[pl.ds(st,win)],acc.at[slot],load_sem.at[slot])
    def core(s,sign,t):
        zz,conds=cond_of(s,sign)
        slot=t*ns+zz
        st=floor_of(plan,flip(other,omasks,obits,t,ph),zz)
        return conds,pltpu.make_async_remote_copy(src_ref=g.at[pl.ds(st,win)],dst_ref=rc.at[slot],
            send_sem=core_send.at[slot],recv_sem=core_recv.at[slot],device_id=(other,z),device_id_type=MESH)
    for e in order:
        conds,cp=load(*e)
        guard(conds,lambda: cp.start())
    pl.semaphore_wait(barrier,len(partners))
    for e in order:
        conds,cp=core(*e)
        guard(conds,lambda: cp.start())
    sends=[]
    def send(conds,slot,dst,rsem,dev):
        i=len(sends)
        cp=pltpu.make_async_remote_copy(src_ref=acc.at[slot],dst_ref=dst,send_sem=send_sem.at[i],recv_sem=rsem,
            device_id=dev,device_id_type=MESH)
        sends.append((conds,cp))
        guard(conds,lambda: cp.start())
    def waiting(conds,dst,rsem):
        cp=pltpu.make_async_remote_copy(src_ref=dst,dst_ref=dst,send_sem=send_sem.at[0],recv_sem=rsem,
            device_id=(di,z),device_id_type=MESH)
        guard(conds,lambda: cp.wait_recv())
    step=2
    def add(dst, slot, parts, final=False):
        @pl.loop(0,win//step)
        def _(i):
            r=pl.ds(i*step,step)
            v=acc[slot,r].astype(jnp.float32)
            for p in parts:
                v=v+p(r).astype(jnp.float32)
            if final: out[r]=v
            else: acc[slot,r]=v.astype(acc.dtype)
    for s,sign,t in order:
        zz,conds=cond_of(s,sign)
        slot=t*ns+zz
        hi_bit=t.bit_length()
        def fn():
            load(s,sign,t)[1].wait()
            waiting([],rc.at[slot],core_recv.at[slot])
            parts=[lambda r: rc[slot,r]]
            for pp in range(hi_bit,ph):
                idx=((1<<pp)-1)*ns+slot
                waiting([],rp.at[idx],ph_recv.at[idx])
                parts.append(lambda r,idx=idx: rp[idx,r])
            add(None,slot,parts,final=False) if not (t==0 and s==0) else add(None,slot,parts,final=True)
        guard(conds,fn)
        if t:
            pp=hi_bit-1
            idx=((1<<pp)-1)*ns+slot-(1<<pp)*ns
            send(conds,slot,rp.at[idx],ph_recv.at[idx],(flip(di,masks,bits,1<<pp,ph),z))
        else:
            def zadd(stream, extra):
                zi=stream*ns+zz
                def fz():
                    waiting([],rz.at[zi],z_recv.at[zi])
                    @pl.loop(0,win//step)
                    def _(i):
                        r=pl.ds(i*step,step)
                        if s==0:
                            out[r]=out[r]+rz[zi,r].astype(jnp.float32)
                        else:
                            acc[slot,r]=(acc[slot,r].astype(jnp.float32)+rz[zi,r].astype(jnp.float32)).astype(acc.dtype)
                guard(conds+extra,fz)
            if sign>=0: zadd(0,[z>0])
            if sign<=0: zadd(1,[z<ns-1])
            if sign>0: send(conds,slot,rz.at[zz],z_recv.at[zz],(di,z+1))
            if sign<0: send(conds,slot,rz.at[ns+zz],z_recv.at[ns+zz],(di,z-1))
    for e in order:
        conds,cp=core(*e)
        guard(conds,lambda: cp.wait_send())
    for conds,cp in sends:
        guard(conds,lambda: cp.wait_send())

def scatter(plan, g):
    win,ns,ph,nslot=plan.win,plan.nseq,plan.phases,plan.slots
    nsend=len(plan.order())
    return pl.pallas_call(
        functools.partial(scatter_kernel,plan),
        out_shape=jax.ShapeDtypeStruct((win,8,LANES),jnp.float32),
        in_specs=[pl.BlockSpec(memory_space=pl.ANY)],
        out_specs=pl.BlockSpec(memory_space=pltpu.VMEM),
        scratch_shapes=[pltpu.VMEM((nslot,win,8,LANES),g.dtype),pltpu.VMEM((nslot,win,8,LANES),g.dtype),
            pltpu.VMEM(((2**ph-1)*ns,win,8,LANES),g.dtype),pltpu.VMEM((2*ns,win,8,LANES),g.dtype),
            pltpu.SemaphoreType.DMA((nslot,)),pltpu.SemaphoreType.DMA((nsend,)),
            pltpu.SemaphoreType.DMA((nslot,)),pltpu.SemaphoreType.DMA((nslot,)),
            pltpu.SemaphoreType.DMA(((2**ph-1)*ns,)),pltpu.SemaphoreType.DMA((2*ns,))],
        compiler_params=pltpu.CompilerParams(collective_id=1,has_side_effects=True,vmem_limit_bytes=48*1024*1024),
        name="scatter_grads",
    )(g)


def weight_kernel(plan, names, places, *refs):
    count = 2 * len(names)
    sources, refs = refs[:count], refs[count:]
    vectors, refs = refs[: len(refs) - count - 4], refs[len(refs) - count - 4 :]
    target, stores, (out, mix, sem) = refs[0], refs[1 : count + 1], refs[count + 1 :]
    loads = []
    for i in range(count):
        loads.append(pltpu.make_async_copy(sources[i], stores[i], sem.at[i]))
        loads[i].start()
    rows = (((0,), (0,)), ((), ()))
    sent = []

    def send(first, tiles):
        if tiles:
            part = pl.ds(first, tiles)
            copy = pltpu.make_async_copy(out.at[part], target.at[part], sem.at[count + len(sent)])
            copy.start()
            sent.append(copy)

    edge = 0
    for name, shape in segments():
        if math.prod(shape) < D * D:
            first = plan.places[name]
            array, begin = places[name]
            for r in range(-(-math.prod(shape) // LANES)):
                line = vectors[array][begin + r : begin + r + 1, :]
                tile, row = divmod(first + r, 8)
                out[tile, row : row + 1, : line.shape[1]] = line.astype(out.dtype)
    for name, shape in segments():
        if math.prod(shape) >= D * D:
            first = plan.places[name] // 8
            send(edge, first - edge)
            edge = first + math.prod(shape) // TILE
    send(edge, plan.total - edge)
    shapes = dict(segments())
    for number, name in enumerate(names):
        shape, first = shapes[name], plan.places[name]
        left, right = stores[2 * number], stores[2 * number + 1]
        wait_all(*loads[2 * number : 2 * number + 2])
        fold = shape[1] // LANES
        step = 256 if fold == 1 else 128

        @pl.loop(0, shape[0] // step)
        def _(i):
            part = left[:, pl.ds(pl.multiple_of(i * step, step), step)]
            value = lax.dot_general(part, right[...], rows, preferred_element_type=jnp.float32)
            if fold > 1:
                for j in range(fold):
                    for lane in range(LANES // 128):
                        at = j * LANES + lane * 128
                        mix[lane, pl.ds(j, step, stride=fold), :] = value[:, at : at + 128]
                value = jnp.concatenate([mix[lane, : step * fold] for lane in range(LANES // 128)], 1)
            tiles = step * fold // 8
            out[pl.ds(first // 8 + i * tiles, tiles)] = value.astype(out.dtype).reshape(tiles, 8, LANES)

        send(first // 8, math.prod(shape) // TILE)
    wait_all(*sent)


def weight_grads(plan, gradients, vectors, places):
    names = list(gradients)
    operands = [value for name in names for value in gradients[name]]
    return pl.pallas_call(
        functools.partial(weight_kernel, plan, names, places),
        out_shape=jax.ShapeDtypeStruct((plan.padded, 8, LANES), jnp.bfloat16),
        in_specs=[ANY_SPEC] * len(operands) + [VMEM_SPEC] * len(vectors),
        out_specs=ANY_SPEC,
        scratch_shapes=[vm(value.shape) for value in operands] + [
            vm((plan.padded, 8, LANES)), vm((LANES // 128, 512, 128), F32),
            DMA((len(operands) + len(segments()),)),
        ],
        compiler_params=pltpu.CompilerParams(vmem_limit_bytes=60 * 1024 * 1024),
        name="weight_grads",
    )(*operands, *vectors)


def bucket_windows(rel_bucket, block_len, count):
    width = -(-(block_len * (count + 1) - 1) // 128) * 128
    padded = jnp.concatenate([rel_bucket, jnp.full((width,), -1, jnp.int32)])
    windows = [padded[(count - 1 - b) * block_len :][:width] for b in range(count)]
    return (jnp.stack(windows)[:, None, :] == jnp.arange(NB, dtype=jnp.int32)[None, :, None]).astype(jnp.float32)


def adam_update(param_vec, grad_in, first_mom, second):
    new_first = BETA_ONE * first_mom + (1.0 - BETA_ONE) * grad_in
    new_second = BETA_TWO * second + (1.0 - BETA_TWO) * grad_in * grad_in
    corr_one = 1.0 - BETA_ONE**STEP
    corr_two = 1.0 - BETA_TWO**STEP
    step_size = new_first / corr_one / (jnp.sqrt(new_second / corr_two) + ADAM_EPS)
    return (param_vec - LEARN_RATE * (step_size + DECAY * param_vec), new_first, new_second)


def unit_rows(values):
    centre = values - jnp.mean(values, -1, keepdims=True)
    scale = lax.rsqrt(jnp.mean(centre * centre, -1, keepdims=True) + NORM_EPS)
    return centre * scale, scale


def unit_back(unit, scale, gain, grad):
    shifted = grad * gain
    first = jnp.mean(shifted, -1, keepdims=True)
    second = jnp.mean(shifted * unit, -1, keepdims=True)
    return scale * (shifted - first - unit * second), total_rows(grad * unit), total_rows(grad)


def total_rows(values):
    return jnp.sum(values, 0, keepdims=True)


def split_rows(source, mix, target, fold):
    block = mix.shape[1]
    lanes = LANES // 128

    @pl.loop(0, source.shape[0] // block)
    def _(i):
        part = source[pl.ds(pl.multiple_of(i * block, block), block), :].astype(jnp.float32)
        for lane in range(lanes):
            mix[lane] = part[:, lane * 128 : (lane + 1) * 128]
        for j in range(fold):
            rows = [mix[lane, pl.ds(j, block // fold, stride=fold), :] for lane in range(lanes)]
            at = pl.multiple_of(i * (block // fold), block // fold)
            target[j, pl.ds(at, block // fold), :] = jnp.concatenate(rows, 1).astype(target.dtype)


class Fetch:
    def __init__(self, plan, packed, sem):
        self.plan, self.packed, self.sem, self.count = plan, packed, sem, 0

    def __call__(self, name, target):
        row = self.plan.places[name] // 8 * 8
        copy = pltpu.make_async_copy(
            self.packed.at[pl.ds(row, target.shape[0])], target, self.sem.at[self.count]
        )
        self.count += 1
        copy.start()
        return copy


def column(j):
    return pl.ds(pl.multiple_of(j * LANES, LANES), LANES)


def wait_all(*copies):
    for copy in copies:
        copy.wait()


def ffn_first_kernel(plan, x, packed, x_out, n_out, w_out, w_in, w_second, v0, v1, v2, bias, acc, mix, sem):
    fetch = Fetch(plan, packed, sem)
    early = [fetch("first_ng", v0), fetch("first_b_in", v1), fetch("first_b_out", v2)]
    in_copy = fetch("first_w_in", w_in)
    late = [fetch("first_w_out", w_second)]
    wait_all(*early)
    gains, bias_in, tail = v0[...].astype(jnp.float32), v1[...].astype(jnp.float32), v2[...].astype(jnp.float32)
    stream = x[...]
    unit, _ = unit_rows(stream)
    normed = (unit * gains[0:1] + gains[1:2]).astype(jnp.bfloat16)
    in_copy.wait()
    split_rows(w_in, mix, w_out, FF // LANES)
    wait_all(*late)
    n_out[...] = normed
    bias[...] = bias_in
    acc[...] = jnp.zeros(acc.shape, jnp.float32)

    @pl.loop(0, FF // LANES)
    def _(j):
        hidden = forward_dot(n_out[...], w_out[j]) + bias[pl.ds(j, 1), :]
        active = swish_act(hidden).astype(jnp.bfloat16)
        acc[...] += forward_dot(active, w_second[column(j), :])

    stream = x[...] + 0.5 * (acc[...] + tail[0:1])
    x_out[...] = stream
    unit, _ = unit_rows(stream)
    normed = (unit * tail[1:2] + tail[2:3]).astype(jnp.bfloat16)
    n_out[...] = normed


def ffn_first_back_kernel(plan, x, x_one, d_two, d_norm_in, w_in, packed,
                          d_out, a_out, r_out, n_out, h_out, vec_out, w_second, v0, v1, v2, bias, acc, sem):
    fetch = Fetch(plan, packed, sem)
    early = [fetch("first_ng", v0), fetch("first_b_in", v1), fetch("first_b_out", v2)]
    late = fetch("first_w_out", w_second)
    wait_all(*early)
    gains, bias_in, tail = v0[...].astype(jnp.float32), v1[...].astype(jnp.float32), v2[...].astype(jnp.float32)
    unit, scale = unit_rows(x_one[...])
    d_normed = d_norm_in[...].astype(jnp.float32)
    d_norm, gain_grad, shift_grad = unit_back(unit, scale, tail[1:2], d_normed)
    vec_out[0:1] = gain_grad
    vec_out[1:2] = shift_grad
    grad = d_two[...] + d_norm
    half = 0.5 * grad
    vec_out[2:3] = total_rows(half)
    half_b = half.astype(jnp.bfloat16)
    r_out[...] = half_b
    unit, scale = unit_rows(x[...])
    normed = (unit * gains[0:1] + gains[1:2]).astype(jnp.bfloat16)
    n_out[...] = normed
    late.wait()
    bias[...] = bias_in
    acc[...] = jnp.zeros(acc.shape, jnp.float32)
    d_out[...] = grad

    @pl.loop(0, FF // LANES)
    def _(j):
        cols = column(j)
        hidden = forward_dot(n_out[...], w_in[j]) + bias[pl.ds(j, 1), :]
        a_out[:, cols] = swish_act(hidden).astype(jnp.bfloat16)
        d_hidden = back_dot(r_out[...], w_second[cols, :]) * swish_grad(hidden)
        vec_out[pl.ds(5 + j, 1), :] = total_rows(d_hidden)
        d_hidden = d_hidden.astype(jnp.bfloat16)
        h_out[:, cols] = d_hidden
        acc[...] += back_dot(d_hidden, w_in[j])

    unit, scale = unit_rows(x[...])
    d_norm, gain_grad, shift_grad = unit_back(unit, scale, gains[0:1], acc[...])
    vec_out[3:4] = gain_grad
    vec_out[4:5] = shift_grad
    d_out[...] += d_norm


def gate_kernel(plan, ctx, x, valid, packed, x_out, n_out, g_out, u_out, w_out, w_o, w_pi, v0, v1, mix, sem):
    fetch = Fetch(plan, packed, sem)
    early = [fetch("w_o", w_o), fetch("b_o", v0), fetch("b_pi", v1)]
    late = fetch("w_pi", w_pi)
    wait_all(*early)
    rows, bias_in = v0[...].astype(jnp.float32), v1[...].astype(jnp.float32)
    stream = x[...] + forward_dot(ctx[...], w_o[...]) + rows[0:1]
    x_out[...] = stream
    unit, _ = unit_rows(stream)
    normed = (unit * rows[6:7] + rows[7:8]).astype(jnp.bfloat16)
    n_out[...] = normed
    late.wait()
    split_rows(w_pi, mix, w_out, 2)
    linear = forward_dot(normed, w_out[0]) + bias_in[0:1]
    gate = forward_dot(normed, w_out[1]) + bias_in[1:2]
    g_out[:, :D] = linear
    g_out[:, D:] = gate
    u_out[...] = linear * jax.nn.sigmoid(gate) * valid[...]


def gate_back_kernel(plan, du, pre_gate, x, d_three, valid, w_pi, packed,
                     g_out, d_out, o_out, c_out, vec_out, w_o, v0, sem):
    fetch = Fetch(plan, packed, sem)
    copies = [fetch("b_o", v0), fetch("w_o", w_o)]
    d_gated = du[...] * valid[...]
    gate_sig = jax.nn.sigmoid(pre_gate[:, D:])
    d_linear = d_gated * gate_sig
    d_gate = d_gated * pre_gate[:, :D] * gate_sig * (1.0 - gate_sig)
    vec_out[0:1] = total_rows(d_linear)
    vec_out[1:2] = total_rows(d_gate)
    d_linear, d_gate = d_linear.astype(jnp.bfloat16), d_gate.astype(jnp.bfloat16)
    g_out[:, :D] = d_linear
    g_out[:, D:] = d_gate
    d_normed = back_dot(d_linear, w_pi[0]) + back_dot(d_gate, w_pi[1])
    unit, scale = unit_rows(x[...])
    wait_all(*copies)
    d_norm, gain_grad, shift_grad = unit_back(unit, scale, v0[...].astype(jnp.float32)[6:7], d_normed)
    vec_out[2:3] = gain_grad
    vec_out[3:4] = shift_grad
    grad = d_three[...] + d_norm
    d_out[...] = grad
    vec_out[4:5] = total_rows(grad)
    grad_b = grad.astype(jnp.bfloat16)
    o_out[...] = grad_b
    c_out[...] = back_dot(grad_b, w_o[...]).astype(jnp.bfloat16)


def middle_kernel(plan, x, depth, sums, cot, valid, packed,
                  y_out, d_out, z_out, part_out, stat_out, e_out, rb_out, a_out, r_out, n_out, h_out, vec_out,
                  w_po, w_in, w_second, w_mix, held, v_bn, v0, v1, v2, bias, acc, mix, sem):
    fetch = Fetch(plan, packed, sem)
    early = [fetch("b_pi", v_bn), fetch("w_po", w_po), fetch("b_po", v0), fetch("second_b_in", v1)]
    early.append(fetch("second_b_out", v2))
    in_copy = fetch("second_w_in", w_in)
    late = fetch("second_w_out", w_second)
    wait_all(*early)
    base = plan.places["bng"] - plan.places["b_pi"]
    batch, head = v_bn[...].astype(jnp.float32), v0[...].astype(jnp.float32)
    bias_in, tail = v1[...].astype(jnp.float32), v2[...].astype(jnp.float32)
    gain, shift = batch[base : base + 1], batch[base + 1 : base + 2]
    count = sums[2:3]
    mean = sums[0:1] / count
    inv_std = lax.rsqrt(sums[1:2] / count - mean * mean + BATCH_EPS)
    stat_out[0:1] = mean
    stat_out[1:2] = inv_std
    stat_out[2:3] = count
    stat_out[3:8] = jnp.zeros((5, D), jnp.float32)
    standard = (depth[...] - mean) * inv_std
    e_out[...] = swish_act(standard * gain + shift).astype(jnp.bfloat16)
    three = x[...] + forward_dot(e_out[...], w_po[...]) + head[0:1]
    unit, scale = unit_rows(three)
    n_out[...] = (unit * head[1:2] + head[2:3]).astype(jnp.bfloat16)
    in_copy.wait()
    split_rows(w_in, mix, w_mix, FF // LANES)
    late.wait()
    bias[...] = bias_in
    acc[...] = jnp.zeros(acc.shape, jnp.float32)
    d_out[...] = three

    @pl.loop(0, FF // LANES)
    def _(j):
        cols = column(j)
        hidden = forward_dot(n_out[...], w_mix[j]) + bias[pl.ds(j, 1), :]
        held[j] = hidden
        active = swish_act(hidden).astype(jnp.bfloat16)
        a_out[:, cols] = active
        acc[...] += forward_dot(active, w_second[cols, :])

    three = d_out[...]
    four = three + 0.5 * (acc[...] + tail[0:1])
    last, last_scale = unit_rows(four)
    y_out[...] = last * tail[1:2] + tail[2:3]
    grad = cot[...] * valid[...]
    grad, gain_grad, shift_grad = unit_back(last, last_scale, tail[1:2], grad)
    vec_out[0:1] = gain_grad
    vec_out[1:2] = shift_grad
    half = 0.5 * grad
    vec_out[2:3] = total_rows(half)
    r_out[...] = half.astype(jnp.bfloat16)
    acc[...] = jnp.zeros(acc.shape, jnp.float32)
    z_out[...] = grad

    @pl.loop(0, FF // LANES)
    def _(j):
        cols = column(j)
        d_hidden = back_dot(r_out[...], w_second[cols, :]) * swish_grad(held[j])
        vec_out[pl.ds(8 + j, 1), :] = total_rows(d_hidden)
        d_hidden = d_hidden.astype(jnp.bfloat16)
        h_out[:, cols] = d_hidden
        acc[...] += back_dot(d_hidden, w_mix[j])

    unit, scale = unit_rows(d_out[...])
    d_norm, gain_grad, shift_grad = unit_back(unit, scale, head[1:2], acc[...])
    vec_out[3:4] = gain_grad
    vec_out[4:5] = shift_grad
    grad = z_out[...] + d_norm
    d_out[...] = grad
    vec_out[5:6] = total_rows(grad)
    rb_out[...] = grad.astype(jnp.bfloat16)
    standard = (depth[...] - mean) * inv_std
    d_active = back_dot(rb_out[...], w_po[...]) * swish_grad(standard * gain + shift)
    d_gain, d_shift = total_rows(d_active * standard), total_rows(d_active)
    vec_out[6:7] = d_gain
    vec_out[7:8] = d_shift
    vec_out[12:16] = jnp.zeros((4, D), jnp.float32)
    d_standard = d_active * gain * valid[...]
    z_out[...] = d_standard
    part_out[0:1] = total_rows(d_standard)
    part_out[1:2] = total_rows(d_standard * standard)
    part_out[2:8] = jnp.zeros((6, D), jnp.float32)


def group_barrier(ndp, nseq):
    di, z = lax.axis_index(DP), lax.axis_index(SEQ)
    peers = [(di, lax.rem(z + i, nseq)) for i in range(1, nseq)]
    peers = peers + [(lax.rem(di + i, ndp), z) for i in range(1, ndp)]
    barrier = pltpu.get_barrier_semaphore()
    for peer in peers:
        pl.semaphore_signal(barrier, inc=1, device_id=peer, device_id_type=MESH)
    return lambda: pl.semaphore_wait(barrier, len(peers))


def exchange_sum(ndp, nseq, part, line, cross, sems):
    di, z = lax.axis_index(DP), lax.axis_index(SEQ)

    def phase(count, me, target, slots, send, recv):
        copies = []
        for i in range(1, count):
            copy = pltpu.make_async_remote_copy(
                src_ref=part, dst_ref=slots.at[me], send_sem=send.at[i], recv_sem=recv.at[me],
                device_id=target(lax.rem(me + i, count)), device_id_type=MESH,
            )
            copy.start()
            copies.append(copy)
        slots[me] = part[...]
        for i in range(1, count):
            source = lax.rem(me + count - i, count)
            pltpu.make_async_remote_copy(
                src_ref=part, dst_ref=slots.at[source], send_sem=send.at[i], recv_sem=recv.at[source],
                device_id=(di, z), device_id_type=MESH,
            ).wait_recv()
        for copy in copies:
            copy.wait_send()
        total = slots[0]
        for i in range(1, count):
            total = total + slots[i]
        return total

    part[...] = phase(nseq, z, lambda i: (di, i), line, sems[0], sems[1])
    return phase(ndp, di, lambda i: (i, z), cross, sems[2], sems[3])


HALO = 16


class Halo:
    def __init__(self, nseq, buffer, sem):
        di, z = lax.axis_index(DP), lax.axis_index(SEQ)
        rows = buffer.shape[1]
        self.has = (z > 0, z < nseq - 1)

        def copy(source, target, number, to):
            return pltpu.make_async_remote_copy(
                src_ref=buffer.at[:, pl.ds(source, HALO)], dst_ref=buffer.at[:, pl.ds(target, HALO)],
                send_sem=sem.at[number], recv_sem=sem.at[2 + number], device_id=(di, to), device_id_type=MESH,
            )

        self.up = copy(rows - 2 * HALO, 0, 0, lax.rem(z + 1, nseq))
        self.down = copy(HALO, rows - HALO, 1, lax.rem(z + nseq - 1, nseq))
        self.buffer, self.rows = buffer, rows

    def start(self):
        @pl.when(self.has[1])
        def _():
            self.up.start()

        @pl.when(self.has[0])
        def _():
            self.down.start()

    def finish(self):
        empty = jnp.zeros((self.buffer.shape[0], HALO, self.buffer.shape[2]), jnp.float32)

        @pl.when(self.has[0])
        def _():
            self.up.wait_recv()
            self.down.wait_send()

        @pl.when(jnp.logical_not(self.has[0]))
        def _():
            self.buffer[:, :HALO] = empty

        @pl.when(self.has[1])
        def _():
            self.down.wait_recv()
            self.up.wait_send()

        @pl.when(jnp.logical_not(self.has[1]))
        def _():
            self.buffer[:, self.rows - HALO :] = empty


def slide(padded, taps, index, out, length):
    lanes = LANES // 128

    @pl.loop(0, padded.shape[0] * lanes)
    def _(i):
        s, lane = i // lanes, pl.ds(pl.multiple_of(i % lanes * 128, 128), 128)
        total = jnp.zeros((length, 128), jnp.float32)
        for b in range(8):
            part = None
            for a in range(4):
                if 0 < 8 * a + b < K + 1:
                    row = index(8 * a + b)
                    term = taps[row : row + 1, lane] * padded[s, 8 * a : 8 * a + length + 8, lane]
                    part = term if part is None else part + term
            total = total + part[b : b + length]
        out[pl.ds(pl.multiple_of(s * length, length), length), lane] = total


def depth_kernel(plan, u, valid, packed, c_out, sum_out, padded, taps, taps_b, part, line, cross, sem,
                 halo_sem, *sems):
    ndp, nseq = plan.ndp, plan.nseq
    arrived = group_barrier(ndp, nseq)
    length = padded.shape[1] - 2 * HALO
    copy = Fetch(plan, packed, sem)("b_pi", taps_b)
    padded[:, HALO : HALO + length] = u[...].reshape(-1, length, D)
    arrived()
    halo = Halo(nseq, padded, halo_sem)
    halo.start()
    copy.wait()
    taps[...] = taps_b[...].astype(jnp.float32)
    halo.finish()
    base = plan.places["w_depth"] - plan.places["b_pi"]
    slide(padded, taps, lambda i: base + i - 1, c_out, length)
    depth, mask = c_out[...], valid[...]
    value = depth * mask
    part[0:1] = total_rows(value)
    part[1:2] = total_rows(value * depth)
    part[2:3] = jnp.broadcast_to(total_rows(mask), (1, LANES))
    part[3:8] = jnp.zeros((5, LANES), jnp.float32)
    sum_out[...] = exchange_sum(ndp, nseq, part, line, cross, sems)


def depth_back_kernel(plan, dz, depth, stats, local, valid, u_pad, packed, u_out, tap_out,
                      padded, own, taps, taps_b, part, line, cross, sem, halo_sem, *sems):
    ndp, nseq = plan.ndp, plan.nseq
    arrived = group_barrier(ndp, nseq)
    seqs, length = padded.shape[0], padded.shape[1] - 2 * HALO
    copy = Fetch(plan, packed, sem)("b_pi", taps_b)
    part[...] = local[...]
    arrived()
    sums = exchange_sum(ndp, nseq, part, line, cross, sems)
    mean, inv_std, count = stats[0:1], stats[1:2], stats[2:3]
    standard = (depth[...] - mean) * inv_std
    d_depth = valid[...] * inv_std * (dz[...] - sums[0:1] / count - standard * (sums[1:2] / count))
    d_depth = d_depth.reshape(seqs, length, D)
    padded[:, HALO : HALO + length] = d_depth
    halo = Halo(nseq, padded, halo_sem)
    halo.start()
    own[:, :8] = jnp.zeros((seqs, 8, D), jnp.float32)
    own[:, 8 : 8 + length] = d_depth
    own[:, 8 + length :] = jnp.zeros((seqs, 8, D), jnp.float32)
    copy.wait()
    taps[...] = taps_b[...].astype(jnp.float32)
    base = plan.places["w_depth"] - plan.places["b_pi"]

    @pl.loop(0, LANES // 128)
    def _(i):
        lane = pl.ds(pl.multiple_of(i * 128, 128), 128)
        for b in range(8):
            sums_b = [None] * 4
            for s in range(seqs):
                moved = own[s, 8 - b : 8 - b + length + 8, lane]
                for a in range(4):
                    if 0 < 8 * a + b < K + 1:
                        term = total_rows(u_pad[s, 8 * a : 8 * a + length + 8, lane] * moved)
                        sums_b[a] = term if sums_b[a] is None else sums_b[a] + term
            for a in range(4):
                if sums_b[a] is not None:
                    tap_out[8 * a + b - 1 : 8 * a + b, lane] = sums_b[a]
        tap_out[K : K + 1, lane] = jnp.zeros((1, 128), jnp.float32)

    halo.finish()
    slide(padded, taps, lambda i: base + K - i, u_out, length)


def head_scores(q, k, line, valid):
    block, full, width = q.shape[0], k.shape[0], line.shape[1]
    scores = lax.dot_general(q, k, (((1,), (1,)), ((), ())), preferred_element_type=jnp.float32)
    spread = jnp.broadcast_to(line, (block, width))
    bias = pltpu.roll(spread, width - block + 1, 1, stride=1, stride_axis=0)[:, :full]
    return jnp.where(valid, scores * (1.0 / math.sqrt(HD)) + bias, -jnp.inf)


def remote(source, target, send, recv, device):
    return pltpu.make_async_remote_copy(
        src_ref=source, dst_ref=target, send_sem=send, recv_sem=recv, device_id=device, device_id_type=MESH
    )


class Team:
    def __init__(self, plan, seqs):
        self.di, self.z = lax.axis_index(DP), lax.axis_index(SEQ)
        self.count, self.seqs = plan.nseq, seqs
        self.c = self.di % 2
        self.base = self.di - self.c
        self.other = self.base + 1 - self.c
        self.owner = self.base + self.z // seqs
        self.main = self.z // seqs == self.c
        self.slot = self.z % seqs
        self.half = pl.ds(pl.multiple_of(self.c * (D // 2), D // 2), D // 2)

    def enter(self):
        barrier = pltpu.get_barrier_semaphore()
        peers = [(self.other, self.z)]
        for i in range(1, self.count):
            to = lax.rem(self.z + i, self.count)
            peers += [(self.di, to), (self.other, to)]
        for peer in peers:
            pl.semaphore_signal(barrier, inc=1, device_id=peer, device_id_type=MESH)
        return lambda: pl.semaphore_wait(barrier, len(peers))

    def turn(self, i):
        return lax.rem(self.z + i, self.count)


def half_copy(packed, plan, name, team, target, sem):
    copy = pltpu.make_async_copy(packed.at[pl.ds(plan.places[name], D), team.half], target, sem)
    copy.start()
    return copy


def attend_kernel(plan, normed, lengths, tables, packed, ctx_out, all_out, q_out, k_out, v_out, lse_out, len_out,
                  w_q, w_k, w_v, b_q, b_v, held, mine, sem, in_send, relay_send, in_recv, ctx_send, ctx_recv, len_sem):
    seqs, block, _ = normed.shape
    count = plan.nseq
    team = Team(plan, seqs)
    arrived = team.enter()
    fetch = Fetch(plan, packed, sem)
    copies = [fetch("b_q", b_q), fetch("b_v", b_v)]
    for i, (name, target) in enumerate((("w_q", w_q), ("w_k", w_k), ("w_v", w_v))):
        copies.append(half_copy(packed, plan, name, team, target, sem.at[2 + i]))
    arrived()
    c, z = team.c, team.z
    sends = []
    for s in range(seqs):
        to = c * seqs + s
        copy = remote(normed.at[s], all_out.at[z], in_send.at[s], in_recv.at[z], (team.di, to))
        sends.append((to != z, copy))
        pl.when(to != z)(copy.start)
    relays = []
    for i in range(count):
        b = team.turn(i)
        source = normed.at[team.slot] if i == 0 else all_out.at[b]
        relays.append(remote(source, all_out.at[b], relay_send.at[b], in_recv.at[b], (team.other, z)))
    pl.when(team.main)(relays[0].start)
    note = remote(lengths, len_out, len_sem.at[0], len_sem.at[1], (team.other, z))
    pl.when(team.main)(note.start)

    @pl.when(team.main)
    def _():
        all_out[z] = normed[team.slot]
        len_out[...] = lengths[...]

    wait_all(*copies)
    mine[0] = b_q[...].astype(jnp.float32)
    mine[1] = b_v[...].astype(jnp.float32)
    bias_q, bias_v = mine[0, 0:1, team.half], mine[1, 0:1, team.half]
    for i in range(count):
        b = team.turn(i)
        if i == 0:
            pl.when(jnp.logical_not(team.main))(relays[0].wait_recv)
        else:
            relays[i].wait_recv()
            pl.when(team.main)(relays[i].start)
        part = all_out[b]
        at = pl.ds(pl.multiple_of(b * block, block), block)
        q_out[at, :] = (forward_dot(part, w_q[...]) + bias_q).astype(jnp.bfloat16)
        k_out[at, :] = forward_dot(part, w_k[...]).astype(jnp.bfloat16)
        v_out[at, :] = (forward_dot(part, w_v[...]) + bias_v).astype(jnp.bfloat16)
    full = count * block
    pl.when(jnp.logical_not(team.main))(note.wait_recv)
    valid = lax.broadcasted_iota(jnp.int32, (1, full), 1) < len_out[pl.ds(team.slot, 1), :][:, 0:1]
    lane = lax.broadcasted_iota(jnp.int32, (block, 128), 1)

    def back(b):
        return remote(held.at[b], ctx_out.at[team.slot, :, team.half], ctx_send.at[b],
                      ctx_recv.at[team.slot * 2 + c], (team.owner, b))

    @pl.loop(0, count)
    def _(i):
        b = lax.rem(z + 1 + i, count)
        at = pl.ds(pl.multiple_of(b * block, block), block)
        lse = jnp.zeros((block, 128), jnp.float32)
        for h in range(H // 2):
            cols = slice(h * HD, (h + 1) * HD)
            line = tables[b, pl.ds(c * (H // 2) + h, 1), :]
            scores = head_scores(q_out[at, cols], k_out[:, cols], line, valid)
            top = jnp.max(scores, -1, keepdims=True)
            weights = jnp.exp(scores - top)
            total = jnp.sum(weights, -1, keepdims=True)
            probs = (weights * (1.0 / total)).astype(jnp.bfloat16)
            ctx = jnp.dot(probs, v_out[:, cols], preferred_element_type=jnp.float32)
            held[b, :, cols] = ctx.astype(jnp.bfloat16)
            lse = jnp.where(lane == h, top + jnp.log(total), lse)
        lse_out[at, :] = lse
        own = jnp.logical_and(b == z, team.main)

        @pl.when(own)
        def _():
            ctx_out[team.slot, :, team.half] = held[b]

        @pl.when(jnp.logical_not(own))
        def _():
            back(b).start()

    for s in range(seqs):
        for h in range(2):
            own = jnp.logical_and(c * seqs + s == z, c == h)
            here = ctx_out.at[s, :, pl.ds(h * (D // 2), D // 2)]
            copy = remote(held.at[0], here, ctx_send.at[0], ctx_recv.at[s * 2 + h], (team.di, z))
            pl.when(jnp.logical_not(own))(copy.wait_recv)
    pl.when(team.main)(note.wait_send)
    for flag, copy in sends:
        pl.when(flag)(copy.wait_send)
    for i in range(count):
        pl.when(team.main)(relays[i].wait_send)
        b = team.turn(i)
        own = jnp.logical_and(b == z, team.main)
        pl.when(jnp.logical_not(own))(back(b).wait_send)


def attend_back_kernel(plan, d_ctx, q_all, k_all, v_all, lse_all, length, tables, packed,
                       dn_out, dq_out, dk_out, dv_out, dt_out, vec_out,
                       w_q, w_k, w_v, d_in, dq_part, dk_sum, dv_sum, give, take, final, sem,
                       in_send, in_recv, swap_send, swap_recv, dn_send, dn_recv):
    seqs, block, _ = d_ctx.shape
    count = plan.nseq
    full = count * block
    team = Team(plan, seqs)
    arrived = team.enter()
    copies = []
    for i, (name, target) in enumerate((("w_q", w_q), ("w_k", w_k), ("w_v", w_v))):
        copies.append(half_copy(packed, plan, name, team, target, sem.at[i]))
    arrived()
    c, z = team.c, team.z
    sends = []
    for s in range(seqs):
        for h in range(2):
            to = c * seqs + s
            own = jnp.logical_and(to == z, c == h)
            source = d_ctx.at[s, :, pl.ds(h * (D // 2), D // 2)]
            copy = remote(source, d_in.at[z], in_send.at[2 * s + h], in_recv.at[z], (team.base + h, to))
            sends.append((jnp.logical_not(own), copy))
            pl.when(jnp.logical_not(own))(copy.start)

    @pl.when(team.main)
    def _():
        d_in[z] = d_ctx[team.slot, :, team.half]

    dk_sum[...] = jnp.zeros(dk_sum.shape, jnp.float32)
    dv_sum[...] = jnp.zeros(dv_sum.shape, jnp.float32)
    dt_out[...] = jnp.zeros(dt_out.shape, jnp.float32)
    vec_out[...] = jnp.zeros(vec_out.shape, jnp.float32)
    away = pl.ds(pl.multiple_of((1 - c) * (D // 2), D // 2), D // 2)
    for out in (dq_out, dk_out, dv_out):
        out[:, away] = jnp.zeros((full, D // 2), jnp.bfloat16)
    valid = lax.broadcasted_iota(jnp.int32, (1, full), 1) < length[pl.ds(team.slot, 1), :][:, 0:1]
    rows = (((0,), (0,)), ((), ()))
    inv = 1.0 / math.sqrt(HD)

    @pl.loop(0, count)
    def _(i):
        b = lax.rem(z + i, count)
        own = jnp.logical_and(b == z, team.main)
        copy = remote(d_in.at[b], d_in.at[b], in_send.at[0], in_recv.at[b], (team.di, z))
        pl.when(jnp.logical_not(own))(copy.wait_recv)
        at = pl.ds(pl.multiple_of(b * block, block), block)
        totals = []
        for h in range(H // 2):
            cols = slice(h * HD, (h + 1) * HD)
            q, k, v = q_all[at, cols], k_all[:, cols], v_all[:, cols]
            dctx = d_in[b, :, cols]
            line = tables[b, pl.ds(c * (H // 2) + h, 1), :]
            width = line.shape[1]
            scores = head_scores(q, k, line, valid)
            probs = jnp.exp(scores - lse_all[at, h : h + 1])
            d_probs = lax.dot_general(dctx, v, (((1,), (1,)), ((), ())), preferred_element_type=jnp.float32)
            delta = jnp.sum(probs * d_probs, -1, keepdims=True)
            d_scores = probs * (d_probs - delta)
            d_scores_b = d_scores.astype(jnp.bfloat16)
            dq = jnp.dot(d_scores_b, k, preferred_element_type=jnp.float32) * inv
            totals.append(total_rows(dq))
            dk_sum[:, cols] += lax.dot_general(d_scores_b, q, rows, preferred_element_type=jnp.float32)
            dv_sum[:, cols] += lax.dot_general(
                probs.astype(jnp.bfloat16), dctx, rows, preferred_element_type=jnp.float32
            )
            dq_part[at, cols] = dq.astype(jnp.bfloat16)
            wide = jnp.concatenate([d_scores, jnp.zeros((block, width - full), jnp.float32)], 1)
            folded = pltpu.roll(wide[0:8], block - 1, 1)
            for g in range(1, block // 8):
                folded = folded + pltpu.roll(wide[8 * g : 8 * g + 8], block - 1 - 8 * g, 1)
            line = folded[0:1]
            for r in range(1, 8):
                line = line + pltpu.roll(folded[r : r + 1], width - r, 1)
            dt_out[b, pl.ds(c * (H // 2) + h, 1), :] = line
        vec_out[0:1, team.half] += jnp.concatenate(totals, 1)

    vec_out[1:2, team.half] = total_rows(dv_sum[...])
    dk_part = (dk_sum[...] * inv).astype(jnp.bfloat16)
    dk_out[:, team.half] = dk_part
    dv_part = dv_sum[...].astype(jnp.bfloat16)
    dv_out[:, team.half] = dv_part
    dq_out[:, team.half] = dq_part[...]
    wait_all(*copies)

    def partial(b):
        at = pl.ds(pl.multiple_of(b * block, block), block)
        dk_rows, dv_rows = dk_out[at, team.half], dv_out[at, team.half]
        return back_dot(dq_part[at, :], w_q[...]) + back_dot(dk_rows, w_k[...]) + back_dot(dv_rows, w_v[...])

    share = count // 2
    swaps, ends = [], []
    for i in range(share):
        give[i] = partial((1 - c) * share + i).astype(jnp.bfloat16)
        copy = remote(give.at[i], take.at[i], swap_send.at[i], swap_recv.at[i], (team.other, z))
        copy.start()
        swaps.append(copy)
    for i in range(share):
        b = c * share + i
        value = partial(b)
        swaps[i].wait_recv()
        value = (value + take[i].astype(jnp.float32)).astype(jnp.bfloat16)
        final[i] = value
        own = jnp.logical_and(b == z, team.main)
        copy = remote(final.at[i], dn_out.at[team.slot], dn_send.at[i], dn_recv.at[team.slot], (team.owner, b))
        ends.append((jnp.logical_not(own), copy))
        pl.when(jnp.logical_not(own))(copy.start)

        @pl.when(own)
        def _():
            dn_out[team.slot] = final[i]

    for s in range(seqs):
        own = jnp.logical_and(c * seqs + s == z, z // share == c)
        copy = remote(final.at[0], dn_out.at[s], dn_send.at[0], dn_recv.at[s], (team.di, z))
        pl.when(jnp.logical_not(own))(copy.wait_recv)
    for copy in swaps:
        copy.wait_send()
    for flag, copy in sends + ends:
        pl.when(flag)(copy.wait_send)


VMEM_SPEC = pl.BlockSpec(memory_space=pltpu.VMEM)
ANY_SPEC = pl.BlockSpec(memory_space=pl.ANY)


def stage(kernel, plan, operands, packed, outs, scratch, name, number=None):
    params = {}
    if number is not None:
        params = {"collective_id": number, "has_side_effects": True}
    specs = [VMEM_SPEC] * len(operands) + [ANY_SPEC]
    return pl.pallas_call(
        functools.partial(kernel, plan),
        out_shape=[jax.ShapeDtypeStruct(shape, dtype) for shape, dtype in outs],
        in_specs=specs,
        out_specs=[VMEM_SPEC] * len(outs),
        scratch_shapes=scratch,
        compiler_params=pltpu.CompilerParams(vmem_limit_bytes=56 * 1024 * 1024, **params),
        name=name,
    )(*operands, packed)


F32, BF16 = jnp.float32, jnp.bfloat16
DMA = pltpu.SemaphoreType.DMA


def vm(shape, dtype=jnp.bfloat16):
    return pltpu.VMEM(shape, dtype)


def exchange_scratch(plan):
    return [vm((8, D), F32), vm((plan.nseq, 8, D), F32), vm((plan.ndp, 8, D), F32), DMA((1,)), DMA((4,)),
            DMA((plan.nseq,)), DMA((plan.nseq,)), DMA((plan.ndp,)), DMA((plan.ndp,))]


def per_device(inputs, lengths, rel_bucket, params, moment_one, moment_two, cotangent):
    seq_count, block_len, model_width = inputs.shape
    rows = seq_count * block_len
    first_pos = lax.axis_index(SEQ) * block_len
    positions = first_pos + jnp.arange(block_len, dtype=jnp.int32)
    valid_own = positions[None, :] < lengths[:, None]
    valid = valid_own.astype(jnp.float32).reshape(-1, 1)
    onehot = bucket_windows(rel_bucket, block_len, lax.axis_size(SEQ))
    assert 2 * seq_count == lax.axis_size(SEQ)
    length = jnp.broadcast_to(jnp.pad(lengths, (0, 8 - seq_count))[:, None], (8, 128))
    plan = Plan(lax.axis_size(DP), lax.axis_size(SEQ), params.shape[0])
    packed = gather(plan, params).reshape(-1, LANES)
    full, wide = (rows, D), (rows, FF)
    square, tall, group = vm((D, D)), vm((FF, D)), vm((8, D))
    mix = vm((LANES // 128, 256, 128), F32)
    stream0 = inputs.reshape(full)
    stream1, normed2, w_first = stage(
        ffn_first_kernel, plan, [stream0], packed,
        [(full, F32), (full, BF16), ((FF // D, D, D), BF16)],
        [tall, tall, group, group, group, vm((8, D), F32), vm(full, F32), mix, DMA((5,))], "ffn_first",
    )
    table_row = plan.places["rel"]
    rel = packed[table_row : table_row + 1, : NB * H].reshape(NB, H)
    tables = jnp.einsum("nh,bnw->bhw", rel, onehot.astype(BF16), preferred_element_type=F32)
    tall_half, split = (plan.nseq * block_len, D // 2), (plan.nseq, block_len, D // 2)
    local3, all3 = (seq_count, block_len, D), (plan.nseq, block_len, D)
    half, nseq = vm((D, D // 2)), plan.nseq
    context, owned, queries, keys, values, lse, length = stage(
        attend_kernel, plan, [normed2.reshape(local3), length, tables], packed,
        [(local3, BF16), (all3, BF16), (tall_half, BF16), (tall_half, BF16), (tall_half, BF16),
         ((tall_half[0], 128), F32), ((8, 128), jnp.int32)],
        [half, half, half, group, group, vm(split), vm((2, 8, D), F32), DMA((5,)), DMA((seq_count,)), DMA((nseq,)),
         DMA((nseq,)), DMA((nseq,)), DMA((2 * seq_count,)), DMA((2,))], "attend", 4,
    )
    context = context.reshape(full)
    stream2, normed3, pre_gate, gated, w_gate = stage(
        gate_kernel, plan, [context, stream1, valid], packed,
        [(full, F32), (full, BF16), ((rows, 2 * D), F32), (full, F32), ((2, D, D), BF16)],
        [square, vm((2 * D, D)), group, group, mix, DMA((4,))], "gate",
    )
    padded_shape = (seq_count, block_len + 2 * HALO, D)
    depth, sums, padded = stage(
        depth_kernel, plan, [gated, valid], packed,
        [(full, F32), ((8, D), F32), (padded_shape, F32)],
        [vm((40, D), F32), vm((40, D))] + exchange_scratch(plan), "depth", 2,
    )
    (output, d_stream3, d_standard, local, stats, active3, grad3_b, active4, half4, normed4, d_hidden4,
     vec_mid) = stage(
        middle_kernel, plan, [stream2, depth, sums, cotangent.reshape(full), valid], packed,
        [(full, F32), (full, F32), (full, F32), ((8, D), F32), ((8, D), F32), (full, BF16), (full, BF16),
         (wide, BF16), (full, BF16), (full, BF16), (wide, BF16), ((16, D), F32)],
        [square, tall, tall, vm((FF // D, D, D)), vm((FF // D, rows, D), F32), vm((40, D)), group, group, group,
         vm((8, D), F32), vm(full, F32), mix, DMA((7,))], "middle",
    )
    d_gated, tap_grads = stage(
        depth_back_kernel, plan, [d_standard, depth, stats, local, valid, padded], packed,
        [(full, F32), ((32, D), F32)],
        [vm(padded_shape, F32), vm((seq_count, block_len + 16, D), F32), vm((40, D), F32), vm((40, D))]
        + exchange_scratch(plan), "depth_back", 3,
    )
    d_gate, d_stream2, grad2_b, d_context, vec_gate = stage(
        gate_back_kernel, plan, [d_gated, pre_gate, stream2, d_stream3, valid, w_gate], packed,
        [((rows, 2 * D), BF16), (full, F32), (full, BF16), (full, BF16), ((8, D), F32)],
        [square, group, DMA((2,))], "gate_back",
    )
    whole = (tall_half[0], D)
    d_norm2, d_query, d_key, d_value, d_tables, vec_attend = stage(
        attend_back_kernel, plan, [d_context.reshape(local3), queries, keys, values, lse, length, tables], packed,
        [(local3, BF16), (whole, BF16), (whole, BF16), (whole, BF16), (tables.shape, F32), ((8, D), F32)],
        [half, half, half, vm(split), vm(tall_half), vm(tall_half, F32), vm(tall_half, F32),
         vm((nseq // 2, block_len, D)), vm((nseq // 2, block_len, D)), vm((nseq // 2, block_len, D)), DMA((3,)),
         DMA((2 * seq_count,)), DMA((nseq,)), DMA((nseq // 2,)), DMA((nseq // 2,)), DMA((nseq // 2,)),
         DMA((seq_count,))], "attend_back", 5,
    )
    rel_grad = jnp.einsum("bnw,bhw->nh", onehot, d_tables, precision=lax.Precision.HIGHEST).reshape(1, -1)
    owned = owned.reshape(whole)
    d_stream0, active1, half1, normed1, d_hidden1, vec_first = stage(
        ffn_first_back_kernel, plan, [stream0, stream1, d_stream2, d_norm2.reshape(full), w_first], packed,
        [(full, F32), (wide, BF16), (full, BF16), (full, BF16), (wide, BF16), ((16, D), F32)],
        [tall, group, group, group, vm((8, D), F32), vm(full, F32), DMA((4,))], "ffn_first_back",
    )
    gradients = {
        "w_k": (owned, d_key), "w_v": (owned, d_value),
        "first_w_in": (normed1, d_hidden1), "first_w_out": (active1, half1), "w_q": (owned, d_query),
        "w_o": (context, grad2_b), "w_pi": (normed3, d_gate), "w_po": (active3, grad3_b),
        "second_w_in": (normed4, d_hidden4), "second_w_out": (active4, half4),
    }
    places = {
        "attn_ng": (0, 0), "attn_nb": (0, 1), "first_b_out": (0, 2), "first_ng": (0, 3), "first_nb": (0, 4),
        "first_b_in": (0, 5), "b_pi": (1, 0), "conv_ng": (1, 2), "conv_nb": (1, 3), "b_o": (1, 4),
        "fin_g": (2, 0), "fin_b": (2, 1), "second_b_out": (2, 2), "second_ng": (2, 3), "second_nb": (2, 4),
        "b_po": (2, 5), "bng": (2, 6), "bnb": (2, 7), "second_b_in": (2, 8), "w_depth": (3, 0),
        "b_q": (4, 0), "b_v": (4, 1), "rel": (5, 0),
    }
    vectors = [vec_first, vec_gate, vec_mid, tap_grads, vec_attend, rel_grad]
    window = scatter(plan, weight_grads(plan, gradients, vectors, places))
    grad_shard = own_shard(plan, window)
    new_params, new_first, new_second = adam_update(params, grad_shard, moment_one, moment_two)
    return (
        output.reshape(inputs.shape),
        d_stream0.reshape(inputs.shape),
        grad_shard,
        new_params,
        new_first,
        new_second,
    )


def solution(mesh):
    return jax.shard_map(
        per_device,
        mesh=mesh,
        in_specs=(
            P(DP, SEQ, None),
            P(DP),
            P(),
            P((DP, SEQ)),
            P((DP, SEQ)),
            P((DP, SEQ)),
            P(DP, SEQ, None),
        ),
        out_specs=(
            P(DP, SEQ, None),
            P(DP, SEQ, None),
            P((DP, SEQ)),
            P((DP, SEQ)),
            P((DP, SEQ)),
            P((DP, SEQ)),
        ),
        check_vma=False,
    )
```

profile of v0, /device:TPU:9, one launch (start us, length us, event | category | flops | bytes accessed | tf_op | source)
XLA Modules:
  0.0 323.7 jit_solution(3756615462141987403)
XLA Ops:
  0.6 0.7 constant_dynamic-slice_fusion
  2.0 0.7 compare_convert_fusion
  2.7 0.7 fusion.5
  6.6 0.7 broadcast_in_dim.2.lengths
  7.3 0.9 pad_slice_fusion
  8.3 0.9 reshape.112.valid
  9.1 2.0 pad_bitcast_fusion.x
  11.2 62.5 %gather_params.1 = bf16[1486,8,512]{2,1,0:T(8,128)(2,1)} custom-call(f32[1480,128]{1,0:T(8,128)} %pad_bitcast_fusion.x), custom_call_target="tpu_custom_call" | custom-call | tf_op jit(solution)/shard_map/gather_params/pallas_call | solution.py:361
  73.7 0.7 slice_reduce_fusion
  74.5 0.9 convolution_bitcast_fusion.tables
  75.4 8.0 %ffn_first.1 = (f32[384,512]{1,0:T(8,128)}, bf16[384,512]{1,0:T(8,128)(2,1)}, bf16[4,512,512]{2,1,0:T(8,128)(2,1)}) custom-call(f32[384,512]{1,0:T(8,128)} %bitcast.44, bf16[11888,512]{1,0:T(8,128)(2,1)} %bitcast.31), custom_call_target="tpu_custom_call" | custom-call | tf_op jit(solution)/shard_map/ffn_first/pallas_call | solution.py:1302
  83.4 35.3 %attend.1 = (bf16[2,192,512]{2,1,0:T(8,128)(2,1)}, bf16[4,192,512]{2,1,0:T(8,128)(2,1)}, bf16[768,256]{1,0:T(8,128)(2,1)}, bf16[768,256]{1,0:T(8,128)(2,1)}, bf1...) custom-call(bf16[2,192,512]{2,1,0:T(8,128)(2,1)} %bitcast.50, s32[8,128]{1,0:T(8,128)} %broadcast_in_dim.2.lengths, ...), custom_call_target="tpu_custom_call" | custom-call | tf_op jit(solution)/shard_map/attend/pallas_call | solution.py:1302
  118.6 5.6 %gate.1 = (f32[384,512]{1,0:T(8,128)}, bf16[384,512]{1,0:T(8,128)(2,1)}, f32[384,1024]{1,0:T(8,128)}, f32[384,512]{1,0:T(8,128)}, bf16[2,512,512]{2,1,0:T(8,128)(2,1)}) custom-call(bf16[384,512]{1,0:T(8,128)(2,1)} %bitcast.46, f32[384,512]{1,0:T(8,128)} %get-tuple-element.57.x.x_one, f32[384,1]{1,0:T(8,128)} %reshape.112.valid, bf16[11888,512]{1,0:T(8,128)(2,1)} %bitcast.33), custom_call_target="tpu_custom_call" | custom-call | tf_op jit(solution)/shard_map/gate/pallas_call | solution.py:1302
  124.2 19.1 %depth.1 = (f32[384,512]{1,0:T(8,128)}, f32[8,512]{1,0:T(8,128)}, f32[2,224,512]{2,1,0:T(8,128)}) custom-call(f32[384,512]{1,0:T(8,128)} %get-tuple-element.59.u, f32[384,1]{1,0:T(8,128)} %reshape.112.valid, bf16[11888,512]{1,0:T(8,128)(2,1)} %bitcast.34), custom_call_target="tpu_custom_call" | custom-call | tf_op jit(solution)/shard_map/depth/pallas_call | solution.py:1302
  143.3 14.0 %middle.1 = (f32[384,512]{1,0:T(8,128)}, f32[384,512]{1,0:T(8,128)}, f32[384,512]{1,0:T(8,128)}, f32[8,512]{1,0:T(8,128)}, f32[8,512]{1,0:T(8,128)}, /*index=5*/...) custom-call(f32[384,512]{1,0:T(8,128)} %get-tuple-element.58.x, ...), custom_call_target="tpu_custom_call" | custom-call | tf_op jit(solution)/shard_map/middle/pallas_call | solution.py:1302
  157.4 17.5 %depth_back.1 = (f32[384,512]{1,0:T(8,128)}, f32[32,512]{1,0:T(8,128)}) custom-call(f32[384,512]{1,0:T(8,128)} %get-tuple-element.63.dz, f32[384,512]{1,0:T(8,128)} %get-tuple-element.60.depth, f32[8,512]{1,0:T(8,128)} %get-tuple-element.64.stats, f32[8,512]{1,0:T(8,128)} %get-tuple-element.65.local, f32[384,1]{1,0:T(8,128)} %reshape.112.valid, ...), custom_call_target="tpu_custom_call" | custom-call | tf_op jit(solution)/shard_map/depth_back/pallas_call | solution.py:1302
  174.9 5.2 %gate_back.1 = (bf16[384,1024]{1,0:T(8,128)(2,1)}, f32[384,512]{1,0:T(8,128)}, bf16[384,512]{1,0:T(8,128)(2,1)}, bf16[384,512]{1,0:T(8,128)(2,1)}, f32[8,512]{1,0:T(8,128)}) custom-call(f32[384,512]{1,0:T(8,128)} %get-tuple-element.67.du, f32[384,1024]{1,0:T(8,128)} %get-tuple-element.68.pre_gate, f32[384,512]{1,0:T(8,128)} %get-tuple-element.58.x, ...), custom_call_target="tpu_custom_call" | custom-call | tf_op jit(solution)/shard_map/gate_back/pallas_call | solution.py:1302
  180.1 40.4 %attend_back.1 = (bf16[2,192,512]{2,1,0:T(8,128)(2,1)}, bf16[768,512]{1,0:T(8,128)(2,1)}, bf16[768,512]{1,0:T(8,128)(2,1)}, bf16[768,512]{1,0:T(8,128)(2,1)}, f32[4,8,1024]{2,1,0:T(8,128)}, /*index=5*/f32[8,512]{1,0:T(8,128)}) custom-call(bf16[2,192,512]{2,1,0:T(8,128)(2,1)} %bitcast.49, bf16[768,256]{1,0:T(8,128)(2,1)} %get-tuple-element.73.q_all, ...), custom_call_target="tpu_custom_call" | custom-call | tf_op jit(solution)/shard_map/attend_back/pallas_call | solution.py:1302
  220.5 1.3 convolution_bitcast_fusion.1
  222.4 9.5 %ffn_first_back.1 = (f32[384,512]{1,0:T(8,128)}, bf16[384,2048]{1,0:T(8,128)(2,1)}, bf16[384,512]{1,0:T(8,128)(2,1)}, bf16[384,512]{1,0:T(8,128)(2,1)}, bf16[384,2048]{1,0:T(8,128)(2,1)}, /*index=5*/f32[16,512]{1,0:T(8,128)}) custom-call(f32[384,512]{1,0:T(8,128)} %bitcast.45, f32[384,512]{1,0:T(8,128)} %get-tuple-element.57.x.x_one, ...), custom_call_target="tpu_custom_call" | custom-call | tf_op jit(solution)/shard_map/ffn_first_back/pallas_call | solution.py:1302
  231.9 19.2 %weight_grads.1.g = bf16[1487,8,512]{2,1,0:T(8,128)(2,1)} custom-call(bf16[768,512]{1,0:T(8,128)(2,1)} %bitcast.40, bf16[768,512]{1,0:T(8,128)(2,1)} %get-tuple-element.82.refs_1_, bf16[768,512]{1,0:T(8,128)(2,1)} %bitcast.41, bf16[768,512]{1,0:T(8,128)(2,1)} %get-tuple-element.83.refs_3_, bf16[384,512]{1,0:T(8,128)(2,1)} %get-tuple-element.84.refs_4_, ...), custom_call_target="tpu_custom_call" | custom-call | tf_op jit(solution)/shard_map/weight_grads/pallas_call | solution.py:561
  251.1 68.0 %scatter_grads.1 = f32[48,8,512]{2,1,0:T(8,128)S(1)} custom-call(bf16[1487,8,512]{2,1,0:T(8,128)(2,1)} %weight_grads.1.g), custom_call_target="tpu_custom_call" | custom-call | tf_op jit(solution)/shard_map/scatter_grads/pallas_call | solution.py:484
  319.3 0.9 copy-done
  320.4 3.3 %multiply_subtract_fusion = (f32[189368]{0:T(1024)}, f32[189368]{0:T(1024)}, f32[189368]{0:T(1024)}, f32[189368]{0:T(1024)}) fusion(f32[189368]{0:T(1024)S(1)} %copy-done, f32[189368]{0:T(1024)S(1)} %copy-done.1, f32[189368]{0:T(1024)S(1)} %copy-done.2, f32[196608]{0:T(1024)S(1)} %bitcast.43, s32[]{:T(128)S(6)} %select_n.15, s32[]{:T(128)S(6)} %select_n.14, ...), kind=kLoop, calls=%fused_computation.4 | loop fusion | flops 3219256 | bytes 6817260 | tf_op jit(solution)/shard_map/sub | solution.py:588
  (11 shorter events, 1.9 us)
Async XLA Ops:
  251.1 68.2 %copy-start.2 = (f32[189368]{0:T(1024)S(1)}, f32[189368]{0:T(1024)}, u32[]{:S(2)}) copy-start(f32[189368]{0:T(1024)} %param.13) | copy-start | bytes 2272420
  319.1 1.1 copy-start
  319.1 1.3 copy-start.1
where the time goes:
time: 324 us
  Pallas kernels  304 us (94%)
  local copies, waits for them, and re-layouts  9.32 us (3%)
  between operations  4.03 us (1%)
  other arithmetic  4.02 us (1%)
    pallas_call x9, Pallas kernels, stage(): pl.pallas_call(functools.partial(kernel, plan), out_shape=[jax.ShapeDtype...  155 us
    pallas_call x1, Pallas kernels, scatter(): pl.pallas_call(functools.partial(scatter_kernel, plan), out_shape=jax.Sha...  68 us
    pallas_call x1, Pallas kernels, gather(): pl.pallas_call(functools.partial(gather_kernel, plan), out_shape=jax.Shap...  62.5 us
    pallas_call x1, Pallas kernels, weight_grads(): pl.pallas_call(functools.partial(weight_kernel, plan, names, places), out...  19.2 us

commit v1 on v0

--- a/solution.py
+++ b/solution.py
@@ -1,5 +1,6 @@
 import functools
 import math
+import types
 
 import jax
 import jax.numpy as jnp
@@ -643,11 +644,12 @@
         copy.wait()
 
 
-def ffn_first_kernel(plan, x, packed, x_out, n_out, w_out, w_in, w_second, v0, v1, v2, bias, acc, mix, sem):
+def ffn_first_kernel(plan, x, packed, x_out, n_out, w_out, w_in, w_second, v0, v1, v2, bias, acc, one, mix, sem):
     fetch = Fetch(plan, packed, sem)
     early = [fetch("first_ng", v0), fetch("first_b_in", v1), fetch("first_b_out", v2)]
     in_copy = fetch("first_w_in", w_in)
     late = [fetch("first_w_out", w_second)]
+    yield
     wait_all(*early)
     gains, bias_in, tail = v0[...].astype(jnp.float32), v1[...].astype(jnp.float32), v2[...].astype(jnp.float32)
     stream = x[...]
@@ -656,13 +658,13 @@
     in_copy.wait()
     split_rows(w_in, mix, w_out, FF // LANES)
     wait_all(*late)
-    n_out[...] = normed
+    one[...] = normed
     bias[...] = bias_in
     acc[...] = jnp.zeros(acc.shape, jnp.float32)
 
     @pl.loop(0, FF // LANES)
     def _(j):
-        hidden = forward_dot(n_out[...], w_out[j]) + bias[pl.ds(j, 1), :]
+        hidden = forward_dot(one[...], w_out[j]) + bias[pl.ds(j, 1), :]
         active = swish_act(hidden).astype(jnp.bfloat16)
         acc[...] += forward_dot(active, w_second[column(j), :])
 
@@ -670,7 +672,7 @@
     x_out[...] = stream
     unit, _ = unit_rows(stream)
     normed = (unit * tail[1:2] + tail[2:3]).astype(jnp.bfloat16)
-    n_out[...] = normed
+    n_out[...] = normed.reshape(n_out.shape)
 
 
 def ffn_first_back_kernel(plan, x, x_one, d_two, d_norm_in, w_in, packed,
@@ -678,10 +680,11 @@
     fetch = Fetch(plan, packed, sem)
     early = [fetch("first_ng", v0), fetch("first_b_in", v1), fetch("first_b_out", v2)]
     late = fetch("first_w_out", w_second)
+    yield
     wait_all(*early)
     gains, bias_in, tail = v0[...].astype(jnp.float32), v1[...].astype(jnp.float32), v2[...].astype(jnp.float32)
     unit, scale = unit_rows(x_one[...])
-    d_normed = d_norm_in[...].astype(jnp.float32)
+    d_normed = d_norm_in[...].astype(jnp.float32).reshape(-1, D)
     d_norm, gain_grad, shift_grad = unit_back(unit, scale, tail[1:2], d_normed)
     vec_out[0:1] = gain_grad
     vec_out[1:2] = shift_grad
@@ -720,9 +723,10 @@
     fetch = Fetch(plan, packed, sem)
     early = [fetch("w_o", w_o), fetch("b_o", v0), fetch("b_pi", v1)]
     late = fetch("w_pi", w_pi)
+    yield
     wait_all(*early)
     rows, bias_in = v0[...].astype(jnp.float32), v1[...].astype(jnp.float32)
-    stream = x[...] + forward_dot(ctx[...], w_o[...]) + rows[0:1]
+    stream = x[...] + forward_dot(ctx[...].reshape(-1, D), w_o[...]) + rows[0:1]
     x_out[...] = stream
     unit, _ = unit_rows(stream)
     normed = (unit * rows[6:7] + rows[7:8]).astype(jnp.bfloat16)
@@ -740,6 +744,7 @@
                      g_out, d_out, o_out, c_out, vec_out, w_o, v0, sem):
     fetch = Fetch(plan, packed, sem)
     copies = [fetch("b_o", v0), fetch("w_o", w_o)]
+    yield
     d_gated = du[...] * valid[...]
     gate_sig = jax.nn.sigmoid(pre_gate[:, D:])
     d_linear = d_gated * gate_sig
@@ -760,7 +765,7 @@
     vec_out[4:5] = total_rows(grad)
     grad_b = grad.astype(jnp.bfloat16)
     o_out[...] = grad_b
-    c_out[...] = back_dot(grad_b, w_o[...]).astype(jnp.bfloat16)
+    c_out[...] = back_dot(grad_b, w_o[...]).astype(jnp.bfloat16).reshape(c_out.shape)
 
 
 def middle_kernel(plan, x, depth, sums, cot, valid, packed,
@@ -771,6 +776,7 @@
     early.append(fetch("second_b_out", v2))
     in_copy = fetch("second_w_in", w_in)
     late = fetch("second_w_out", w_second)
+    yield
     wait_all(*early)
     base = plan.places["bng"] - plan.places["b_pi"]
     batch, head = v_bn[...].astype(jnp.float32), v0[...].astype(jnp.float32)
@@ -782,7 +788,7 @@
     stat_out[0:1] = mean
     stat_out[1:2] = inv_std
     stat_out[2:3] = count
-    stat_out[3:8] = jnp.zeros((5, D), jnp.float32)
+    stat_out[3:4] = jnp.zeros((1, D), jnp.float32)
     standard = (depth[...] - mean) * inv_std
     e_out[...] = swish_act(standard * gain + shift).astype(jnp.bfloat16)
     three = x[...] + forward_dot(e_out[...], w_po[...]) + head[0:1]
@@ -845,13 +851,16 @@
     z_out[...] = d_standard
     part_out[0:1] = total_rows(d_standard)
     part_out[1:2] = total_rows(d_standard * standard)
-    part_out[2:8] = jnp.zeros((6, D), jnp.float32)
-
-
-def group_barrier(ndp, nseq):
+    part_out[2:4] = jnp.zeros((2, D), jnp.float32)
+
+
+def everyone(plan):
     di, z = lax.axis_index(DP), lax.axis_index(SEQ)
-    peers = [(di, lax.rem(z + i, nseq)) for i in range(1, nseq)]
-    peers = peers + [(lax.rem(di + i, ndp), z) for i in range(1, ndp)]
+    other = di + 1 - 2 * (di % 2)
+    peers = [(lax.rem(di + i, plan.ndp), z) for i in range(1, plan.ndp)]
+    for i in range(1, plan.nseq):
+        to = lax.rem(z + i, plan.nseq)
+        peers += [(di, to), (other, to)]
     barrier = pltpu.get_barrier_semaphore()
     for peer in peers:
         pl.semaphore_signal(barrier, inc=1, device_id=peer, device_id_type=MESH)
@@ -959,11 +968,10 @@
 def depth_kernel(plan, u, valid, packed, c_out, sum_out, padded, taps, taps_b, part, line, cross, sem,
                  halo_sem, *sems):
     ndp, nseq = plan.ndp, plan.nseq
-    arrived = group_barrier(ndp, nseq)
     length = padded.shape[1] - 2 * HALO
     copy = Fetch(plan, packed, sem)("b_pi", taps_b)
+    yield
     padded[:, HALO : HALO + length] = u[...].reshape(-1, length, D)
-    arrived()
     halo = Halo(nseq, padded, halo_sem)
     halo.start()
     copy.wait()
@@ -976,18 +984,17 @@
     part[0:1] = total_rows(value)
     part[1:2] = total_rows(value * depth)
     part[2:3] = jnp.broadcast_to(total_rows(mask), (1, LANES))
-    part[3:8] = jnp.zeros((5, LANES), jnp.float32)
+    part[3:4] = jnp.zeros((1, LANES), jnp.float32)
     sum_out[...] = exchange_sum(ndp, nseq, part, line, cross, sems)
 
 
 def depth_back_kernel(plan, dz, depth, stats, local, valid, u_pad, packed, u_out, tap_out,
                       padded, own, taps, taps_b, part, line, cross, sem, halo_sem, *sems):
     ndp, nseq = plan.ndp, plan.nseq
-    arrived = group_barrier(ndp, nseq)
     seqs, length = padded.shape[0], padded.shape[1] - 2 * HALO
     copy = Fetch(plan, packed, sem)("b_pi", taps_b)
+    yield
     part[...] = local[...]
-    arrived()
     sums = exchange_sum(ndp, nseq, part, line, cross, sems)
     mean, inv_std, count = stats[0:1], stats[1:2], stats[2:3]
     standard = (depth[...] - mean) * inv_std
@@ -1049,16 +1056,6 @@
         self.slot = self.z % seqs
         self.half = pl.ds(pl.multiple_of(self.c * (D // 2), D // 2), D // 2)
 
-    def enter(self):
-        barrier = pltpu.get_barrier_semaphore()
-        peers = [(self.other, self.z)]
-        for i in range(1, self.count):
-            to = lax.rem(self.z + i, self.count)
-            peers += [(self.di, to), (self.other, to)]
-        for peer in peers:
-            pl.semaphore_signal(barrier, inc=1, device_id=peer, device_id_type=MESH)
-        return lambda: pl.semaphore_wait(barrier, len(peers))
-
     def turn(self, i):
         return lax.rem(self.z + i, self.count)
 
@@ -1074,12 +1071,11 @@
     seqs, block, _ = normed.shape
     count = plan.nseq
     team = Team(plan, seqs)
-    arrived = team.enter()
     fetch = Fetch(plan, packed, sem)
     copies = [fetch("b_q", b_q), fetch("b_v", b_v)]
     for i, (name, target) in enumerate((("w_q", w_q), ("w_k", w_k), ("w_v", w_v))):
         copies.append(half_copy(packed, plan, name, team, target, sem.at[2 + i]))
-    arrived()
+    yield
     c, z = team.c, team.z
     sends = []
     for s in range(seqs):
@@ -1177,11 +1173,10 @@
     count = plan.nseq
     full = count * block
     team = Team(plan, seqs)
-    arrived = team.enter()
     copies = []
     for i, (name, target) in enumerate((("w_q", w_q), ("w_k", w_k), ("w_v", w_v))):
         copies.append(half_copy(packed, plan, name, team, target, sem.at[i]))
-    arrived()
+    yield
     c, z = team.c, team.z
     sends = []
     for s in range(seqs):
@@ -1294,20 +1289,66 @@
 ANY_SPEC = pl.BlockSpec(memory_space=pl.ANY)
 
 
-def stage(kernel, plan, operands, packed, outs, scratch, name, number=None):
-    params = {}
-    if number is not None:
-        params = {"collective_id": number, "has_side_effects": True}
-    specs = [VMEM_SPEC] * len(operands) + [ANY_SPEC]
-    return pl.pallas_call(
-        functools.partial(kernel, plan),
-        out_shape=[jax.ShapeDtypeStruct(shape, dtype) for shape, dtype in outs],
-        in_specs=specs,
+def run_all(ready, runs, first):
+    for run in runs:
+        next(run)
+    for number, run in enumerate(runs):
+        if number == first:
+            ready()
+        for _ in run:
+            pass
+
+
+def forward_kernel(plan, r):
+    ready = everyone(plan)
+    runs = [
+        ffn_first_kernel(plan, r.x, r.packed, r.x1, r.n2, r.w_first, r.w_in, r.w_second, r.g0, r.g1, r.g2, r.bias,
+                         r.acc, r.one, r.mix, r.sem0),
+        attend_kernel(plan, r.n2, r.lengths, r.tables, r.packed, r.ctx, r.owned, r.q, r.k, r.v, r.lse, r.length,
+                      r.w_q, r.w_k, r.w_v, r.g3, r.g4, r.held, r.mine, r.sem1, r.sem2, r.sem3, r.sem4, r.sem5, r.sem6,
+                      r.sem7),
+        gate_kernel(plan, r.ctx, r.x1, r.valid, r.packed, r.x2, r.n3, r.gates, r.u, r.w_gate, r.w_o, r.w_pi,
+                    r.g5, r.g6, r.mix, r.sem8),
+        depth_kernel(plan, r.u, r.valid, r.packed, r.depth, r.sums, r.padded, r.taps, r.taps_b, r.part, r.line,
+                     r.cross, r.sem9, r.sem10, r.sem11, r.sem12, r.sem13, r.sem14),
+    ]
+    run_all(ready, runs, 1)
+
+
+def backward_kernel(plan, r):
+    ready = everyone(plan)
+    runs = [
+        middle_kernel(plan, r.x2, r.depth, r.sums, r.cot, r.valid, r.packed, r.y, r.d3, r.dz, r.local, r.stats, r.e3,
+                      r.r3, r.a4, r.h4, r.n4, r.dh4, r.vec_mid, r.w_po, r.w_in, r.w_second, r.w_mix, r.hid, r.g0,
+                      r.g1, r.g2, r.g3, r.bias, r.acc, r.mix, r.sem0),
+        depth_back_kernel(plan, r.dz, r.depth, r.stats, r.local, r.valid, r.padded, r.packed, r.du, r.tap, r.wide,
+                          r.own, r.taps, r.taps_b, r.part, r.line, r.cross, r.sem1, r.sem2, r.sem3, r.sem4, r.sem5,
+                          r.sem6),
+        gate_back_kernel(plan, r.du, r.gates, r.x2, r.d3, r.valid, r.w_gate, r.packed, r.dg, r.d2, r.r2, r.dctx,
+                         r.vec_gate, r.w_o, r.g4, r.sem7),
+        attend_back_kernel(plan, r.dctx, r.q, r.k, r.v, r.lse, r.length, r.tables, r.packed, r.dn, r.dq, r.dk, r.dv,
+                           r.dt, r.vec_att, r.w_q, r.w_k, r.w_v, r.d_in, r.dq_part, r.dk_sum, r.dv_sum, r.give, r.take,
+                           r.final, r.sem8, r.sem9, r.sem10, r.sem11, r.sem12, r.sem13, r.sem14),
+        ffn_first_back_kernel(plan, r.x, r.x1, r.d2, r.dn, r.w_first, r.packed, r.d0, r.a1, r.h1, r.n1, r.dh1,
+                              r.vec_first, r.w_tall, r.g5, r.g6, r.g7, r.bias, r.acc, r.sem15),
+    ]
+    run_all(ready, runs, 1)
+
+
+def stage(kernel, plan, operands, packed, outs, scratch, name, number):
+    keys = list(operands) + ["packed"] + list(outs) + list(scratch)
+    results = pl.pallas_call(
+        lambda *refs: kernel(plan, types.SimpleNamespace(**dict(zip(keys, refs)))),
+        out_shape=[jax.ShapeDtypeStruct(shape, dtype) for shape, dtype in outs.values()],
+        in_specs=[VMEM_SPEC] * len(operands) + [ANY_SPEC],
         out_specs=[VMEM_SPEC] * len(outs),
-        scratch_shapes=scratch,
-        compiler_params=pltpu.CompilerParams(vmem_limit_bytes=56 * 1024 * 1024, **params),
+        scratch_shapes=list(scratch.values()),
+        compiler_params=pltpu.CompilerParams(
+            vmem_limit_bytes=67043328, collective_id=number, has_side_effects=True
+        ),
         name=name,
-    )(*operands, packed)
+    )(*operands.values(), packed)
+    return types.SimpleNamespace(**dict(zip(outs, results)))
 
 
 F32, BF16 = jnp.float32, jnp.bfloat16
@@ -1316,11 +1357,6 @@
 
 def vm(shape, dtype=jnp.bfloat16):
     return pltpu.VMEM(shape, dtype)
-
-
-def exchange_scratch(plan):
-    return [vm((8, D), F32), vm((plan.nseq, 8, D), F32), vm((plan.ndp, 8, D), F32), DMA((1,)), DMA((4,)),
-            DMA((plan.nseq,)), DMA((plan.nseq,)), DMA((plan.ndp,)), DMA((plan.ndp,))]
 
 
 def per_device(inputs, lengths, rel_bucket, params, moment_one, moment_two, cotangent):
@@ -1335,80 +1371,62 @@
     length = jnp.broadcast_to(jnp.pad(lengths, (0, 8 - seq_count))[:, None], (8, 128))
     plan = Plan(lax.axis_size(DP), lax.axis_size(SEQ), params.shape[0])
     packed = gather(plan, params).reshape(-1, LANES)
-    full, wide = (rows, D), (rows, FF)
+    full, wide, nseq = (rows, D), (rows, FF), plan.nseq
     square, tall, group = vm((D, D)), vm((FF, D)), vm((8, D))
-    mix = vm((LANES // 128, 256, 128), F32)
-    stream0 = inputs.reshape(full)
-    stream1, normed2, w_first = stage(
-        ffn_first_kernel, plan, [stream0], packed,
-        [(full, F32), (full, BF16), ((FF // D, D, D), BF16)],
-        [tall, tall, group, group, group, vm((8, D), F32), vm(full, F32), mix, DMA((5,))], "ffn_first",
-    )
+    mix, taps, taps_b = vm((LANES // 128, 256, 128), F32), vm((40, D), F32), vm((40, D))
+    half, sums = vm((D, D // 2)), ((4, D), F32)
+    long, whole = nseq * block_len, (nseq * block_len, D)
+    local3, split = (seq_count, block_len, D), (nseq, block_len, D // 2)
+    padded = (seq_count, block_len + 2 * HALO, D)
+    few = vm((nseq // 2, block_len, D))
+    x = inputs.reshape(full)
     table_row = plan.places["rel"]
     rel = packed[table_row : table_row + 1, : NB * H].reshape(NB, H)
     tables = jnp.einsum("nh,bnw->bhw", rel, onehot.astype(BF16), preferred_element_type=F32)
-    tall_half, split = (plan.nseq * block_len, D // 2), (plan.nseq, block_len, D // 2)
-    local3, all3 = (seq_count, block_len, D), (plan.nseq, block_len, D)
-    half, nseq = vm((D, D // 2)), plan.nseq
-    context, owned, queries, keys, values, lse, length = stage(
-        attend_kernel, plan, [normed2.reshape(local3), length, tables], packed,
-        [(local3, BF16), (all3, BF16), (tall_half, BF16), (tall_half, BF16), (tall_half, BF16),
-         ((tall_half[0], 128), F32), ((8, 128), jnp.int32)],
-        [half, half, half, group, group, vm(split), vm((2, 8, D), F32), DMA((5,)), DMA((seq_count,)), DMA((nseq,)),
-         DMA((nseq,)), DMA((nseq,)), DMA((2 * seq_count,)), DMA((2,))], "attend", 4,
+    f = stage(
+        forward_kernel, plan, dict(x=x, valid=valid, lengths=length, tables=tables), packed,
+        dict(x1=(full, F32), w_first=((FF // D, D, D), BF16), ctx=(local3, BF16), owned=((nseq, block_len, D), BF16),
+             q=((long, D // 2), BF16), k=((long, D // 2), BF16), v=((long, D // 2), BF16), lse=((long, 128), F32),
+             length=((8, 128), jnp.int32), x2=(full, F32), n3=(full, BF16), gates=((rows, 2 * D), F32),
+             w_gate=((2, D, D), BF16), depth=(full, F32), sums=sums, padded=(padded, F32)),
+        dict(n2=vm(local3), w_in=tall, w_second=tall, g0=group, g1=group, g2=group, g3=group, g4=group, g5=group,
+             g6=group, bias=vm((8, D), F32), acc=vm(full, F32), one=vm(full), mix=mix, w_q=half, w_k=half, w_v=half,
+             held=vm(split), mine=vm((2, 8, D), F32), u=vm(full, F32), w_o=square, w_pi=vm((2 * D, D)), taps=taps,
+             taps_b=taps_b, part=vm(*sums), line=vm((nseq, 4, D), F32), cross=vm((plan.ndp, 4, D), F32),
+             sem0=DMA((5,)), sem1=DMA((5,)), sem2=DMA((seq_count,)), sem3=DMA((nseq,)), sem4=DMA((nseq,)),
+             sem5=DMA((nseq,)), sem6=DMA((2 * seq_count,)), sem7=DMA((2,)), sem8=DMA((4,)), sem9=DMA((1,)),
+             sem10=DMA((4,)), sem11=DMA((nseq,)), sem12=DMA((nseq,)), sem13=DMA((plan.ndp,)),
+             sem14=DMA((plan.ndp,))), "forward", 2,
     )
-    context = context.reshape(full)
-    stream2, normed3, pre_gate, gated, w_gate = stage(
-        gate_kernel, plan, [context, stream1, valid], packed,
-        [(full, F32), (full, BF16), ((rows, 2 * D), F32), (full, F32), ((2, D, D), BF16)],
-        [square, vm((2 * D, D)), group, group, mix, DMA((4,))], "gate",
+    b = stage(
+        backward_kernel, plan,
+        dict(x=x, valid=valid, cot=cotangent.reshape(full), tables=tables, x1=f.x1, x2=f.x2, depth=f.depth,
+             sums=f.sums, padded=f.padded, gates=f.gates, w_gate=f.w_gate, q=f.q, k=f.k, v=f.v, lse=f.lse,
+             length=f.length, w_first=f.w_first), packed,
+        dict(y=(full, F32), d0=(full, F32), e3=(full, BF16), r3=(full, BF16), a4=(wide, BF16), h4=(full, BF16),
+             n4=(full, BF16), dh4=(wide, BF16), vec_mid=((16, D), F32), tap=((32, D), F32), dg=((rows, 2 * D), BF16),
+             r2=(full, BF16), vec_gate=((8, D), F32), dq=(whole, BF16), dk=(whole, BF16), dv=(whole, BF16),
+             dt=(tables.shape, F32), vec_att=((8, D), F32), a1=(wide, BF16), h1=(full, BF16), n1=(full, BF16),
+             dh1=(wide, BF16), vec_first=((16, D), F32)),
+        dict(d3=vm(full, F32), dz=vm(full, F32), local=vm(*sums), stats=vm(*sums), w_po=square, w_in=tall,
+             w_second=tall, w_mix=vm((FF // D, D, D)), hid=vm((FF // D, rows, D), F32), g0=vm((40, D)), g1=group,
+             g2=group, g3=group, g4=group, g5=group, g6=group, g7=group, bias=vm((8, D), F32), acc=vm(full, F32),
+             mix=mix, du=vm(full, F32), wide=vm(padded, F32), own=vm((seq_count, block_len + 16, D), F32), taps=taps,
+             taps_b=taps_b, part=vm(*sums), line=vm((nseq, 4, D), F32), cross=vm((plan.ndp, 4, D), F32),
+             d2=vm(full, F32), dctx=vm(local3), w_o=square, dn=vm(local3), w_q=half, w_k=half, w_v=half,
+             d_in=vm(split), dq_part=vm((long, D // 2)), dk_sum=vm((long, D // 2), F32),
+             dv_sum=vm((long, D // 2), F32), give=few, take=few, final=few, w_tall=tall, sem0=DMA((7,)),
+             sem1=DMA((1,)), sem2=DMA((4,)), sem3=DMA((nseq,)), sem4=DMA((nseq,)), sem5=DMA((plan.ndp,)),
+             sem6=DMA((plan.ndp,)), sem7=DMA((2,)), sem8=DMA((3,)), sem9=DMA((2 * seq_count,)), sem10=DMA((nseq,)),
+             sem11=DMA((nseq // 2,)), sem12=DMA((nseq // 2,)), sem13=DMA((nseq // 2,)), sem14=DMA((seq_count,)),
+             sem15=DMA((4,))), "backward", 3,
     )
-    padded_shape = (seq_count, block_len + 2 * HALO, D)
-    depth, sums, padded = stage(
-        depth_kernel, plan, [gated, valid], packed,
-        [(full, F32), ((8, D), F32), (padded_shape, F32)],
-        [vm((40, D), F32), vm((40, D))] + exchange_scratch(plan), "depth", 2,
-    )
-    (output, d_stream3, d_standard, local, stats, active3, grad3_b, active4, half4, normed4, d_hidden4,
-     vec_mid) = stage(
-        middle_kernel, plan, [stream2, depth, sums, cotangent.reshape(full), valid], packed,
-        [(full, F32), (full, F32), (full, F32), ((8, D), F32), ((8, D), F32), (full, BF16), (full, BF16),
-         (wide, BF16), (full, BF16), (full, BF16), (wide, BF16), ((16, D), F32)],
-        [square, tall, tall, vm((FF // D, D, D)), vm((FF // D, rows, D), F32), vm((40, D)), group, group, group,
-         vm((8, D), F32), vm(full, F32), mix, DMA((7,))], "middle",
-    )
-    d_gated, tap_grads = stage(
-        depth_back_kernel, plan, [d_standard, depth, stats, local, valid, padded], packed,
-        [(full, F32), ((32, D), F32)],
-        [vm(padded_shape, F32), vm((seq_count, block_len + 16, D), F32), vm((40, D), F32), vm((40, D))]
-        + exchange_scratch(plan), "depth_back", 3,
-    )
-    d_gate, d_stream2, grad2_b, d_context, vec_gate = stage(
-        gate_back_kernel, plan, [d_gated, pre_gate, stream2, d_stream3, valid, w_gate], packed,
-        [((rows, 2 * D), BF16), (full, F32), (full, BF16), (full, BF16), ((8, D), F32)],
-        [square, group, DMA((2,))], "gate_back",
-    )
-    whole = (tall_half[0], D)
-    d_norm2, d_query, d_key, d_value, d_tables, vec_attend = stage(
-        attend_back_kernel, plan, [d_context.reshape(local3), queries, keys, values, lse, length, tables], packed,
-        [(local3, BF16), (whole, BF16), (whole, BF16), (whole, BF16), (tables.shape, F32), ((8, D), F32)],
-        [half, half, half, vm(split), vm(tall_half), vm(tall_half, F32), vm(tall_half, F32),
-         vm((nseq // 2, block_len, D)), vm((nseq // 2, block_len, D)), vm((nseq // 2, block_len, D)), DMA((3,)),
-         DMA((2 * seq_count,)), DMA((nseq,)), DMA((nseq // 2,)), DMA((nseq // 2,)), DMA((nseq // 2,)),
-         DMA((seq_count,))], "attend_back", 5,
-    )
-    rel_grad = jnp.einsum("bnw,bhw->nh", onehot, d_tables, precision=lax.Precision.HIGHEST).reshape(1, -1)
-    owned = owned.reshape(whole)
-    d_stream0, active1, half1, normed1, d_hidden1, vec_first = stage(
-        ffn_first_back_kernel, plan, [stream0, stream1, d_stream2, d_norm2.reshape(full), w_first], packed,
-        [(full, F32), (wide, BF16), (full, BF16), (full, BF16), (wide, BF16), ((16, D), F32)],
-        [tall, group, group, group, vm((8, D), F32), vm(full, F32), DMA((4,))], "ffn_first_back",
-    )
+    rel_grad = jnp.einsum("bnw,bhw->nh", onehot, b.dt, precision=lax.Precision.HIGHEST).reshape(1, -1)
+    owned = f.owned.reshape(whole)
     gradients = {
-        "w_k": (owned, d_key), "w_v": (owned, d_value),
-        "first_w_in": (normed1, d_hidden1), "first_w_out": (active1, half1), "w_q": (owned, d_query),
-        "w_o": (context, grad2_b), "w_pi": (normed3, d_gate), "w_po": (active3, grad3_b),
-        "second_w_in": (normed4, d_hidden4), "second_w_out": (active4, half4),
+        "w_k": (owned, b.dk), "w_v": (owned, b.dv), "w_q": (owned, b.dq), "second_w_in": (b.n4, b.dh4),
+        "second_w_out": (b.a4, b.h4), "w_pi": (f.n3, b.dg), "w_po": (b.e3, b.r3), "w_o": (f.ctx.reshape(full), b.r2),
+        "first_w_in": (b.n1, b.dh1), "first_w_out": (b.a1, b.h1),
     }
     places = {
         "attn_ng": (0, 0), "attn_nb": (0, 1), "first_b_out": (0, 2), "first_ng": (0, 3), "first_nb": (0, 4),
@@ -1417,13 +1435,13 @@
         "b_po": (2, 5), "bng": (2, 6), "bnb": (2, 7), "second_b_in": (2, 8), "w_depth": (3, 0),
         "b_q": (4, 0), "b_v": (4, 1), "rel": (5, 0),
     }
-    vectors = [vec_first, vec_gate, vec_mid, tap_grads, vec_attend, rel_grad]
+    vectors = [b.vec_first, b.vec_gate, b.vec_mid, b.tap, b.vec_att, rel_grad]
     window = scatter(plan, weight_grads(plan, gradients, vectors, places))
     grad_shard = own_shard(plan, window)
     new_params, new_first, new_second = adam_update(params, grad_shard, moment_one, moment_two)
     return (
-        output.reshape(inputs.shape),
-        d_stream0.reshape(inputs.shape),
+        b.y.reshape(inputs.shape),
+        b.d0.reshape(inputs.shape),
         grad_shard,
         new_params,
         new_first,

time: 324 us -> 298 us (0.920)
  Pallas kernels: 304 us -> 278 us
    pallas_call x9 -> x2, Pallas kernels: 155 us -> 128 us  [stage(): pl.pallas_call(lambda *refs: kernel(plan, types.SimpleNamespace(**dict(zi...]
where the time goes in v1:
time: 298 us
  Pallas kernels  278 us (93%)
  local copies, waits for them, and re-layouts  9.92 us (3%)
  between operations  4.01 us (1%)
  other arithmetic  3.41 us (1%)
    pallas_call x2, Pallas kernels, stage(): pl.pallas_call(lambda *refs: kernel(plan, types.SimpleNamespace(**dict(zi...  128 us
    pallas_call x1, Pallas kernels, scatter(): pl.pallas_call(functools.partial(scatter_kernel, plan), out_shape=jax.Sha...  68.3 us
    pallas_call x1, Pallas kernels, gather(): pl.pallas_call(functools.partial(gather_kernel, plan), out_shape=jax.Shap...  62.5 us
    pallas_call x1, Pallas kernels, weight_grads(): pl.pallas_call(functools.partial(weight_kernel, plan, names, places), out...  19.6 us

profile of v1, /device:TPU:9, one launch (start us, length us, event | category | flops | bytes accessed | tf_op | source)
XLA Modules:
  0.0 297.8 jit_solution(17896163321123590526)
XLA Ops:
  0.6 0.9 pad_slice_fusion
  1.6 0.0 copy-start.5
  1.6 2.0 pad_bitcast_fusion.x
  3.6 62.5 %gather_params.1 = bf16[1486,8,512]{2,1,0:T(8,128)(2,1)} custom-call(f32[1480,128]{1,0:T(8,128)} %pad_bitcast_fusion.x), custom_call_target="tpu_custom_call" | custom-call | tf_op jit(solution)/shard_map/gather_params/pallas_call | solution.py:362
  66.2 0.7 slice_reduce_fusion
  66.9 0.1 reshape.90
  67.0 0.9 convolution_bitcast_fusion.refs_3_
  67.9 0.1 compare_convert_fusion
  67.9 0.9 reshape.100.refs_1_
  68.8 0.7 broadcast_in_dim.2.refs_2_
  69.5 55.2 %forward.1 = (f32[384,512]{1,0:T(8,128)}, bf16[4,512,512]{2,1,0:T(8,128)(2,1)}, bf16[2,192,512]{2,1,0:T(8,128)(2,1)}, bf16[4,192,512]{2,1,0:T(8,128)(2,1)}, bf16...) custom-call(f32[384,512]{1,0:T(8,128)} %bitcast.34, ...), custom_call_target="tpu_custom_call" | custom-call | tf_op jit(solution)/shard_map/forward/pallas_call | solution.py:1340
  124.7 72.7 %backward.1 = (f32[384,512]{1,0:T(8,128)}, f32[384,512]{1,0:T(8,128)}, bf16[384,512]{1,0:T(8,128)(2,1)}, bf16[384,512]{1,0:T(8,128)(2,1)}, bf16[384,2048]{1,0:T(...) custom-call(f32[384,512]{1,0:T(8,128)} %bitcast.35, ...), custom_call_target="tpu_custom_call" | custom-call | tf_op jit(solution)/shard_map/backward/pallas_call | solution.py:1340
  197.4 1.3 convolution_bitcast_fusion.1
  198.7 0.7 reshape.95.refs_25_
  199.3 19.6 %weight_grads.1.g = bf16[1487,8,512]{2,1,0:T(8,128)(2,1)} custom-call(bf16[768,512]{1,0:T(8,128)(2,1)} %bitcast.30, bf16[768,512]{1,0:T(8,128)(2,1)} %get-tuple-element.61.refs_1_, bf16[768,512]{1,0:T(8,128)(2,1)} %bitcast.31, bf16[768,512]{1,0:T(8,128)(2,1)} %get-tuple-element.62.refs_3_, bf16[768,512]{1,0:T(8,128)(2,1)} %bitcast.32, ...), custom_call_target="tpu_custom_call" | custom-call | tf_op jit(solution)/shard_map/weight_grads/pallas_call | solution.py:562
  219.0 0.0 copy-start.4
  219.0 68.3 %scatter_grads.1 = f32[48,8,512]{2,1,0:T(8,128)S(1)} custom-call(bf16[1487,8,512]{2,1,0:T(8,128)(2,1)} %weight_grads.1.g), custom_call_target="tpu_custom_call" | custom-call | tf_op jit(solution)/shard_map/scatter_grads/pallas_call | solution.py:485
  287.3 0.2 copy.24
  287.5 0.8 constant_dynamic-slice_fusion
  288.4 0.6 fusion.5
  292.2 3.3 %multiply_subtract_fusion = (f32[189368]{0:T(1024)}, f32[189368]{0:T(1024)}, f32[189368]{0:T(1024)}, f32[189368]{0:T(1024)}) fusion(f32[189368]{0:T(1024)S(1)} %copy-done, f32[189368]{0:T(1024)S(1)} %copy-done.3, f32[189368]{0:T(1024)S(1)} %copy-done.4, f32[196608]{0:T(1024)S(1)} %bitcast.33, s32[]{:T(128)S(6)} %select_n.15, s32[]{:T(128)S(6)} %select_n.14, ...), kind=kLoop, calls=%fused_computation.4 | loop fusion | flops 3219256 | bytes 6817260 | tf_op jit(solution)/shard_map/sub | solution.py:589
  295.6 0.9 copy.27
  296.4 0.5 copy-done.1
  297.0 0.9 copy.28
  (14 shorter events, 0.1 us)
Async XLA Ops:
  1.6 65.4 %copy-start.5 = (s32[4,1024]{1,0:T(4,128)}, s32[4,1024]{1,0:T(4,128)S(1)}, u32[]{:S(2)}) copy-start(s32[4,1024]{1,0:T(4,128)S(1)} %pad_add_fusion) | copy-start | bytes 49156
  3.6 64.2 %copy-start.6 = (s32[2]{0:T(128)S(1)}, s32[2]{0:T(128)}, u32[]{:S(2)}) copy-start(s32[2]{0:T(128)} %param.9) | copy-start | bytes 28
  219.0 73.2 %copy-start.4 = (f32[189368]{0:T(1024)S(1)}, f32[189368]{0:T(1024)}, u32[]{:S(2)}) copy-start(f32[189368]{0:T(1024)} %param.13) | copy-start | bytes 2272420
  287.3 4.9 %copy-start = (f32[189368]{0:T(1024)S(1)}, f32[189368]{0:T(1024)}, u32[]{:S(2)}) copy-start(f32[189368]{0:T(1024)} %param.11) | copy-start | bytes 2272420
  287.3 4.9 %copy-start.3 = (f32[189368]{0:T(1024)S(1)}, f32[189368]{0:T(1024)}, u32[]{:S(2)}) copy-start(f32[189368]{0:T(1024)} %param.12) | copy-start | bytes 2272420
  292.2 3.3 %copy-start.2 = (f32[384,512]{1,0:T(8,128)S(1)}, f32[384,512]{1,0:T(8,128)}, u32[]{:S(2)}) copy-start(f32[384,512]{1,0:T(8,128)} %get-tuple-element.58) | copy-start | bytes 2359300
  295.5 1.4 copy-start.1

commit v2 on v1

--- a/solution.py
+++ b/solution.py
@@ -213,7 +213,7 @@
         block[part, :, j * 128 : (j + 1) * 128] = value.reshape(rows // 8, 8, 128)
 
 
-def gather_kernel(plan, x, out, src, line, rolled, give, take, near_sem, send_a, send_b, recv_a, recv_b, loc_sem):
+def gather_kernel(plan, x, out, src, line, rolled, give, take, near_sem, send_a, recv_a, loc_sem):
     di, z = lax.axis_index(DP), lax.axis_index(SEQ)
     ns, ph = plan.nseq, plan.phases
     c = di%2
@@ -255,103 +255,158 @@
         device_id=(before // ns, lax.rem(before, ns)),device_id_type=MESH)
     near.start()
 
-    def pair(ref, base, dst_start, size, sidx, ridx, dev):
-        copies=[pltpu.make_async_remote_copy(src_ref=ref.at[pl.ds(base,lo)],dst_ref=out.at[pl.ds(dst_start,lo)],
-            send_sem=send_a.at[sidx],recv_sem=recv_a.at[ridx],device_id=dev,device_id_type=MESH)]
-        for x in range(more):
-            copies.append(pltpu.make_async_remote_copy(src_ref=ref.at[pl.ds(base+lo+x,1)],dst_ref=out.at[pl.ds(dst_start+lo+x,1)],
-                send_sem=send_b.at[sidx*more+x],recv_sem=recv_b.at[ridx*more+x],device_id=dev,device_id_type=MESH))
+    pieces = gather_pieces(plan)
+    number = sum(len(p) for p in pieces)
+    last = len(pieces) - 1
+    used = [0]
+
+    def pair(kind, ref, base, target, size, ridx, dev, fresh):
+        copies = []
+        for x, (at, tiles) in enumerate(pieces[kind]):
+            copies.append(pltpu.make_async_remote_copy(
+                src_ref=ref.at[pl.ds(base + at, tiles)], dst_ref=out.at[pl.ds(target + at, tiles)],
+                send_sem=send_a.at[used[0] if fresh else 0], recv_sem=recv_a.at[ridx * number + kind + x],
+                device_id=dev, device_id_type=MESH))
+            used[0] += fresh
         return copies, size
+
     def each(p, act, part=None):
-        for x,copy in enumerate(p[0]):
-            if part is not None and (x==0) != (part==0): continue
-            if x<2: act(copy)
+        for x, copy in enumerate(p[0]):
+            if part is not None and (x == 0) != (part == 0):
+                continue
+            if x < 2:
+                act(copy)
             else:
-                @pl.when(p[1]>=lo+x)
-                def _(): act(copy)
-    def start(p,part): each(p, lambda c: c.start(), part)
-    def wait_send(p): each(p, lambda c: c.wait_send())
-    def wait_recv(p,part=None): each(p, lambda c: c.wait_recv(), part)
-
-    own=[pltpu.make_async_copy(src.at[pl.ds(0,lo)],out.at[pl.ds(start_own,lo)],loc_sem.at[0])]
-    for x in range(more):
-        own.append(pltpu.make_async_copy(src.at[pl.ds(lo+x,1)],out.at[pl.ds(start_own+lo+x,1)],loc_sem.at[1+x]))
-    own=(own,size_own)
-    own[0][0].start()
+                pl.when(p[1] >= lo + x)(functools.partial(act, copy))
+
+    def guard(conds, fn):
+        if not conds:
+            fn()
+            return
+        cond = conds[0]
+        for x in conds[1:]:
+            cond = jnp.logical_and(cond, x)
+        pl.when(cond)(fn)
+
+    own = []
+    for at, tiles in sum(pieces, []):
+        own.append(pltpu.make_async_copy(src.at[pl.ds(at, tiles)], out.at[pl.ds(start_own + at, tiles)],
+                                         loc_sem.at[len(own)]))
+
+    def mine_each(act, part):
+        for x, copy in enumerate(own):
+            if (x <= last) != (part == 0):
+                continue
+            if x <= last + 1:
+                act(copy)
+            else:
+                pl.when(size_own >= lo + x - last)(functools.partial(act, copy))
+
+    mine_each(lambda c: c.start(), 0)
+
     def finish_block():
         near.wait_recv()
         at = FRONT + joint
-        line[at:at+1] = line[at:at+1] + take[0:1]
-        line[at+1:at+NEAR] = take[1:]
+        line[at : at + 1] = line[at : at + 1] + take[0:1]
+        line[at + 1 : at + NEAR] = take[1:]
         low = at // 8 * 8
         rolled[low:] = pltpu.roll(line[low:], turn, 1)
-        place_rows(plan, rolled, src, 8*lo, 8*more, lead, cut, skip)
-        for x,copy in enumerate(own[0][1:]):
-            if x==0: copy.start()
-            else:
-                @pl.when(size_own>lo+x)
-                def _(): copy.start()
-    nslot=plan.slots
-    sends=[]
-    def guard(conds, fn):
-        if not conds: fn(); return
-        cond=conds[0]
-        for x in conds[1:]: cond=jnp.logical_and(cond,x)
-        @pl.when(cond)
-        def _(): fn()
-
-    tasks=[]
+        place_rows(plan, rolled, src, 8 * lo, 8 * more, lead, cut, skip)
+        mine_each(lambda c: c.start(), 1)
+
+    nslot = plan.slots
+    sends, tasks = [], []
+    events = [(s + 0.5 * bin(t).count("1") + ROUTES[kind][2], kind, s, sign, t)
+              for kind in range(len(pieces)) for s, sign, t in plan.order()]
+    events.sort()
+    blocks = {}
     for s, sign, t in plan.order():
-        zz = z+sign*s
-        conds=[] if s==0 else ([zz>=0] if sign<0 else [zz<ns])
-        dpi=flip(di,masks,bits,t,ph)
-        st,size=block_of(plan,dpi,zz)
-        mine = s==0 and t==0
+        zz = z + sign * s
+        blocks[s, sign, t] = (block_of(plan, flip(di, masks, bits, t, ph), zz),
+                              block_of(plan, flip(other, omasks, obits, t, ph), zz))
+    for _, kind, s, sign, t in events:
+        zz = z + sign * s
+        conds = [] if s == 0 else ([zz >= 0] if sign < 0 else [zz < ns])
+        st, size = blocks[s, sign, t][0]
+        mine = s == 0 and t == 0
         ref, base = (src, 0) if mine else (out, st)
-        slot = t*ns+zz
-        got = None if mine else pair(out,st,st,size,0,slot,(di,z))
-        copies=[]
+        slot = t * ns + zz
+        got = None if mine else pair(kind, out, st, st, size, slot, (di, z), 0)
+        copies = []
+
         def forward(conds, ridx, dev):
-            p=pair(ref,base,st,size,len(sends),ridx,dev)
-            sends.append((conds,p))
-            copies.append((conds,p))
-        if t==0:
-            if sign<=0 : forward(conds+[z<ns-1],slot,(di,z+1))
-            if sign>=0 : forward(conds+[z>0],slot,(di,z-1))
-        for pp in range(t.bit_length(),ph):
-            forward(conds,slot+(1<<pp)*ns,(flip(di,masks,bits,1<<pp,ph),z))
-        forward(conds,nslot+slot,(other,z))
-        tasks.append((conds,got,copies))
-    def run(task,part):
-        conds,got,copies=task
+            p = pair(kind, ref, base, st, size, ridx, dev, 1)
+            sends.append((conds, p))
+            copies.append((conds, p))
+
+        plane = ROUTES[kind][1]
+        if t == 0 or plane:
+            if sign <= 0:
+                forward(conds + [z < ns - 1], slot, (di, lax.rem(z + 1, ns)))
+            if sign >= 0:
+                forward(conds + [z > 0], slot, (di, lax.rem(z + ns - 1, ns)))
+        if s == 0 or not plane:
+            for pp in range(t.bit_length(), ph):
+                forward(conds, slot + (1 << pp) * ns, (flip(di, masks, bits, 1 << pp, ph), z))
+        forward(conds, nslot + slot, (other, z))
+        tasks.append((kind, conds, got, copies))
+
+    def run(task, part):
+        kind, conds, got, copies = task
+        if part and kind != last:
+            return
         if got is None:
-            if part==1: finish_block()
+            if part:
+                finish_block()
         else:
-            guard(conds, lambda: wait_recv(got,part))
-        for also,p in copies:
-            guard(also, lambda: start(p,part))
-    lag=4
-    for i in range(len(tasks)+lag):
-        if i<len(tasks): run(tasks[i],0)
-        if i>=lag: run(tasks[i-lag],1)
-    for s, sign, t in plan.order():
-        zz=z+sign*s
-        conds=[] if s==0 else ([zz>=0] if sign<0 else [zz<ns])
-        dpi=flip(other,omasks,obits,t,ph)
-        st,size=block_of(plan,dpi,zz)
-        p=pair(out,st,st,size,0,nslot+t*ns+zz,(di,z))
-        guard(conds,lambda: wait_recv(p))
-    for conds,p in sends:
-        guard(conds,lambda: wait_send(p))
-    each(own, lambda c: c.wait())
+            guard(conds, lambda: each(got, lambda c: c.wait_recv(), part))
+        for also, p in copies:
+            guard(also, lambda: each(p, lambda c: c.start(), part))
+
+    lag = 8
+    for i in range(len(tasks) + lag):
+        if i < len(tasks):
+            run(tasks[i], 0)
+        if i >= lag:
+            run(tasks[i - lag], 1)
+    for _, kind, s, sign, t in events:
+        zz = z + sign * s
+        conds = [] if s == 0 else ([zz >= 0] if sign < 0 else [zz < ns])
+        st, size = blocks[s, sign, t][1]
+        p = pair(kind, out, st, st, size, nslot + t * ns + zz, (di, z), 0)
+        guard(conds, lambda: each(p, lambda c: c.wait_recv()))
+    for conds, p in sends:
+        guard(conds, lambda: each(p, lambda c: c.wait_send()))
+    for part in range(2):
+        mine_each(lambda c: c.wait(), part)
     near.wait_send()
 
+
+ROUTES = ((0.39, 0, 0.0), (0.39, 0, 0.3), (0.22, 1, 0.6))
+
+
+def gather_pieces(plan):
+    lo, more = plan.lo - 1, plan.hi - plan.lo + 1
+    pieces, at, share = [], 0, 0.0
+    for part, _, _ in ROUTES:
+        share += part
+        until = lo if len(pieces) == len(ROUTES) - 1 else round(share * plan.lo)
+        pieces.append([(at, until - at)])
+        at = until
+    pieces[-1] += [(lo + x, 1) for x in range(more)]
+    return pieces
+
+
 def count_sends(plan):
-    n=0
-    for s,sign,t in plan.order():
-        if t==0: n+= (2 if sign==0 else 1)
-        n+=plan.phases-t.bit_length()+1
-    return n
+    pieces = gather_pieces(plan)
+    total = 0
+    for kind, (_, plane, _) in enumerate(ROUTES):
+        for s, sign, t in plan.order():
+            along = (2 if s == 0 else 1) if t == 0 or plane else 0
+            across = plan.phases - t.bit_length() if s == 0 or not plane else 0
+            total += (along + across + 1) * len(pieces[kind])
+    return total
+
 
 def gather(plan, params):
     ns, more = count_sends(plan), plan.hi - plan.lo + 1
@@ -368,131 +423,191 @@
             pltpu.VMEM((plan.hi, 8, LANES), jnp.bfloat16), pltpu.VMEM((lines, 128), jnp.float32),
             pltpu.VMEM((lines, 128), jnp.float32), pltpu.VMEM((NEAR, 128), jnp.float32),
             pltpu.VMEM((NEAR, 128), jnp.float32), pltpu.SemaphoreType.DMA((2,)),
-            pltpu.SemaphoreType.DMA((ns,)), pltpu.SemaphoreType.DMA((ns * more,)),
-            pltpu.SemaphoreType.DMA((2 * plan.slots,)), pltpu.SemaphoreType.DMA((2 * plan.slots * more,)),
-            pltpu.SemaphoreType.DMA((1 + more,)),
+            pltpu.SemaphoreType.DMA((ns,)), pltpu.SemaphoreType.DMA((2 * plan.slots * (len(ROUTES) + more),)),
+            pltpu.SemaphoreType.DMA((len(ROUTES) + more,)),
         ],
         compiler_params=pltpu.CompilerParams(collective_id=0, has_side_effects=True),
         name="gather_params",
     )(values)
 
 
-def scatter_kernel(plan, g, out, acc, rc, rp, rz, load_sem, send_sem, core_send, core_recv, ph_recv, z_recv):
+def scatter_pieces(plan):
+    pieces, at, share = [], 0, 0.0
+    for number, (part, _, _) in enumerate(ROUTES):
+        share += part
+        until = plan.win if number == len(ROUTES) - 1 else round(share * plan.win / 2) * 2
+        pieces.append((at, until - at))
+        at = until
+    return pieces
+
+
+def scatter_kernel(plan, g, out, acc, rc, *refs):
+    kinds = len(ROUTES)
+    pieces = scatter_pieces(plan)
+    rps, rzs = refs[:kinds], refs[kinds : 2 * kinds]
+    load_sem, send_sem, core_send, core_recv, ph_recv, z_recv = refs[2 * kinds :]
     di, z = lax.axis_index(DP), lax.axis_index(SEQ)
-    ns, ph, win, nslot = plan.nseq, plan.phases, plan.win, plan.slots
-    c = di%2
+    ns, ph, nslot = plan.nseq, plan.phases, plan.slots
+    c = di % 2
     masks, bits = phase_masks(di, c, ph)
-    other = di+1-2*c
-    omasks, obits = phase_masks(other, 1-c, ph)
-    up, down = lax.rem(z+1,ns), lax.rem(z+ns-1,ns)
-    partners=[(di,up),(di,down),(other,z)]+[(flip(di,masks,bits,1<<p,ph),z) for p in range(ph)]
-    barrier=pltpu.get_barrier_semaphore()
-    for a,b in partners:
-        pl.semaphore_signal(barrier,inc=1,device_id=(a,b),device_id_type=MESH)
-    order=list(reversed(plan.order()))
-    def cond_of(s,sign):
-        zz=z+sign*s
-        return zz,([] if s==0 else ([zz>=0] if sign<0 else [zz<ns]))
+    other = di + 1 - 2 * c
+    omasks, obits = phase_masks(other, 1 - c, ph)
+    up, down = lax.rem(z + 1, ns), lax.rem(z + ns - 1, ns)
+    partners = [(di, up), (di, down), (other, z)] + [(flip(di, masks, bits, 1 << p, ph), z) for p in range(ph)]
+    barrier = pltpu.get_barrier_semaphore()
+    for partner in partners:
+        pl.semaphore_signal(barrier, inc=1, device_id=partner, device_id_type=MESH)
+    order = [(s + 0.5 * bin(t).count("1") + ROUTES[kind][2], kind, s, sign, t)
+             for kind in range(kinds) for s, sign, t in plan.order()]
+    order = [event[1:] for event in sorted(order, reverse=True)]
+
     def guard(conds, fn):
-        if not conds: fn(); return
-        cond=conds[0]
-        for x in conds[1:]: cond=jnp.logical_and(cond,x)
-        @pl.when(cond)
-        def _(): fn()
-    def load(s,sign,t):
-        zz,conds=cond_of(s,sign)
-        slot=t*ns+zz
-        st=floor_of(plan,flip(di,masks,bits,t,ph),zz)
-        return conds,pltpu.make_async_copy(g.at[pl.ds(st,win)],acc.at[slot],load_sem.at[slot])
-    def core(s,sign,t):
-        zz,conds=cond_of(s,sign)
-        slot=t*ns+zz
-        st=floor_of(plan,flip(other,omasks,obits,t,ph),zz)
-        return conds,pltpu.make_async_remote_copy(src_ref=g.at[pl.ds(st,win)],dst_ref=rc.at[slot],
-            send_sem=core_send.at[slot],recv_sem=core_recv.at[slot],device_id=(other,z),device_id_type=MESH)
-    for e in order:
-        conds,cp=load(*e)
-        guard(conds,lambda: cp.start())
-    pl.semaphore_wait(barrier,len(partners))
-    for e in order:
-        conds,cp=core(*e)
-        guard(conds,lambda: cp.start())
-    sends=[]
-    def send(conds,slot,dst,rsem,dev):
-        i=len(sends)
-        cp=pltpu.make_async_remote_copy(src_ref=acc.at[slot],dst_ref=dst,send_sem=send_sem.at[i],recv_sem=rsem,
-            device_id=dev,device_id_type=MESH)
-        sends.append((conds,cp))
-        guard(conds,lambda: cp.start())
-    def waiting(conds,dst,rsem):
-        cp=pltpu.make_async_remote_copy(src_ref=dst,dst_ref=dst,send_sem=send_sem.at[0],recv_sem=rsem,
-            device_id=(di,z),device_id_type=MESH)
-        guard(conds,lambda: cp.wait_recv())
-    step=2
-    def add(dst, slot, parts, final=False):
-        @pl.loop(0,win//step)
-        def _(i):
-            r=pl.ds(i*step,step)
-            v=acc[slot,r].astype(jnp.float32)
-            for p in parts:
-                v=v+p(r).astype(jnp.float32)
-            if final: out[r]=v
-            else: acc[slot,r]=v.astype(acc.dtype)
-    for s,sign,t in order:
-        zz,conds=cond_of(s,sign)
-        slot=t*ns+zz
-        hi_bit=t.bit_length()
-        def fn():
-            load(s,sign,t)[1].wait()
-            waiting([],rc.at[slot],core_recv.at[slot])
-            parts=[lambda r: rc[slot,r]]
-            for pp in range(hi_bit,ph):
-                idx=((1<<pp)-1)*ns+slot
-                waiting([],rp.at[idx],ph_recv.at[idx])
-                parts.append(lambda r,idx=idx: rp[idx,r])
-            add(None,slot,parts,final=False) if not (t==0 and s==0) else add(None,slot,parts,final=True)
-        guard(conds,fn)
-        if t:
-            pp=hi_bit-1
-            idx=((1<<pp)-1)*ns+slot-(1<<pp)*ns
-            send(conds,slot,rp.at[idx],ph_recv.at[idx],(flip(di,masks,bits,1<<pp,ph),z))
-        else:
-            def zadd(stream, extra):
-                zi=stream*ns+zz
-                def fz():
-                    waiting([],rz.at[zi],z_recv.at[zi])
-                    @pl.loop(0,win//step)
-                    def _(i):
-                        r=pl.ds(i*step,step)
-                        if s==0:
-                            out[r]=out[r]+rz[zi,r].astype(jnp.float32)
-                        else:
-                            acc[slot,r]=(acc[slot,r].astype(jnp.float32)+rz[zi,r].astype(jnp.float32)).astype(acc.dtype)
-                guard(conds+extra,fz)
-            if sign>=0: zadd(0,[z>0])
-            if sign<=0: zadd(1,[z<ns-1])
-            if sign>0: send(conds,slot,rz.at[zz],z_recv.at[zz],(di,z+1))
-            if sign<0: send(conds,slot,rz.at[ns+zz],z_recv.at[ns+zz],(di,z-1))
-    for e in order:
-        conds,cp=core(*e)
-        guard(conds,lambda: cp.wait_send())
-    for conds,cp in sends:
-        guard(conds,lambda: cp.wait_send())
+        if not conds:
+            fn()
+            return
+        cond = conds[0]
+        for x in conds[1:]:
+            cond = jnp.logical_and(cond, x)
+        pl.when(cond)(fn)
+
+    def where(kind, s, sign, t):
+        zz = z + sign * s
+        conds = [] if s == 0 else ([zz >= 0] if sign < 0 else [zz < ns])
+        return zz, conds, t * ns + zz
+
+    begins = {}
+    for s, sign, t in plan.order():
+        zz = z + sign * s
+        begins[s, sign, t] = (floor_of(plan, flip(di, masks, bits, t, ph), zz),
+                              floor_of(plan, flip(other, omasks, obits, t, ph), zz))
+
+    def load(kind, s, sign, t):
+        zz, conds, slot = where(kind, s, sign, t)
+        at, tiles = pieces[kind]
+        first = begins[s, sign, t][0] + at
+        return conds, pltpu.make_async_copy(
+            g.at[pl.ds(first, tiles)], acc.at[slot, pl.ds(at, tiles)], load_sem.at[kind * nslot + slot])
+
+    def core(kind, s, sign, t):
+        zz, conds, slot = where(kind, s, sign, t)
+        at, tiles = pieces[kind]
+        first = begins[s, sign, t][1] + at
+        return conds, pltpu.make_async_remote_copy(
+            src_ref=g.at[pl.ds(first, tiles)], dst_ref=rc.at[slot, pl.ds(at, tiles)],
+            send_sem=core_send.at[kind * nslot + slot], recv_sem=core_recv.at[kind * nslot + slot],
+            device_id=(other, z), device_id_type=MESH)
+
+    for event in order:
+        conds, copy = load(*event)
+        guard(conds, copy.start)
+    pl.semaphore_wait(barrier, len(partners))
+    for event in order:
+        conds, copy = core(*event)
+        guard(conds, copy.start)
+    sends = []
+
+    def send(conds, source, target, recv, device):
+        copy = pltpu.make_async_remote_copy(
+            src_ref=source, dst_ref=target, send_sem=send_sem.at[len(sends)], recv_sem=recv,
+            device_id=device, device_id_type=MESH)
+        sends.append((conds, copy))
+        guard(conds, copy.start)
+
+    def waiting(target, recv):
+        pltpu.make_async_remote_copy(
+            src_ref=target, dst_ref=target, send_sem=send_sem.at[0], recv_sem=recv,
+            device_id=(di, z), device_id_type=MESH).wait_recv()
+
+    for event in order:
+        kind, s, sign, t = event
+        zz, conds, slot = where(*event)
+        at, tiles = pieces[kind]
+        plane, rp, rz = ROUTES[kind][1], rps[kind], rzs[kind]
+        final = s == 0 and t == 0
+        high = t.bit_length()
+
+        def combine():
+            part = acc.at[slot, pl.ds(at, tiles)]
+            pltpu.make_async_copy(g.at[pl.ds(0, tiles)], part, load_sem.at[kind * nslot + slot]).wait()
+            waiting(rc.at[slot, pl.ds(at, tiles)], core_recv.at[kind * nslot + slot])
+            sources = []
+            if s == 0 or not plane:
+                for pp in range(high, ph):
+                    entry = ((1 << pp) - 1) * ns + slot
+                    waiting(rp.at[entry], ph_recv.at[kind * nslot + entry])
+                    sources.append(entry)
+
+            @pl.loop(0, tiles // 2)
+            def _(i):
+                here, there = pl.ds(at + i * 2, 2), pl.ds(i * 2, 2)
+                value = acc[slot, here].astype(jnp.float32) + rc[slot, here].astype(jnp.float32)
+                for entry in sources:
+                    value = value + rp[entry, there].astype(jnp.float32)
+                if final:
+                    out[here] = value
+                else:
+                    acc[slot, here] = value.astype(acc.dtype)
+
+        guard(conds, combine)
+
+        def along(stream, extra):
+            entry = (t * 2 + stream) * ns + zz
+
+            def merge():
+                waiting(rz.at[entry], z_recv.at[kind * 2 * nslot + entry])
+
+                @pl.loop(0, tiles // 2)
+                def _(i):
+                    here, there = pl.ds(at + i * 2, 2), pl.ds(i * 2, 2)
+                    if final:
+                        out[here] = out[here] + rz[entry, there].astype(jnp.float32)
+                    else:
+                        value = acc[slot, here].astype(jnp.float32) + rz[entry, there].astype(jnp.float32)
+                        acc[slot, here] = value.astype(acc.dtype)
+
+            guard(conds + extra, merge)
+
+        chained = t == 0 or plane
+        if chained:
+            if sign >= 0:
+                along(0, [z > 0])
+            if sign <= 0:
+                along(1, [z < ns - 1])
+        source = acc.at[slot, pl.ds(at, tiles)]
+        if chained and s:
+            stream = 0 if sign > 0 else 1
+            entry = (t * 2 + stream) * ns + zz
+            send(conds, source, rz.at[entry], z_recv.at[kind * 2 * nslot + entry], (di, up if sign > 0 else down))
+        elif t:
+            pp = high - 1
+            entry = ((1 << pp) - 1) * ns + slot - (1 << pp) * ns
+            send(conds, source, rp.at[entry], ph_recv.at[kind * nslot + entry],
+                 (flip(di, masks, bits, 1 << pp, ph), z))
+    for event in order:
+        conds, copy = core(*event)
+        guard(conds, copy.wait_send)
+    for conds, copy in sends:
+        guard(conds, copy.wait_send)
+
 
 def scatter(plan, g):
-    win,ns,ph,nslot=plan.win,plan.nseq,plan.phases,plan.slots
-    nsend=len(plan.order())
+    win, nslot, kinds = plan.win, plan.slots, len(ROUTES)
+    buffers = []
+    for at, tiles in scatter_pieces(plan):
+        buffers.append(pltpu.VMEM(((2**plan.phases - 1) * plan.nseq, tiles, 8, LANES), g.dtype))
+    for (_, plane, _), (at, tiles) in zip(ROUTES, scatter_pieces(plan)):
+        buffers.append(pltpu.VMEM((2 * nslot if plane else 2 * plan.nseq, tiles, 8, LANES), g.dtype))
+    counts = (kinds * nslot, kinds * len(plan.order()), kinds * nslot, kinds * nslot, kinds * nslot, kinds * 2 * nslot)
     return pl.pallas_call(
-        functools.partial(scatter_kernel,plan),
-        out_shape=jax.ShapeDtypeStruct((win,8,LANES),jnp.float32),
+        functools.partial(scatter_kernel, plan),
+        out_shape=jax.ShapeDtypeStruct((win, 8, LANES), jnp.float32),
         in_specs=[pl.BlockSpec(memory_space=pl.ANY)],
         out_specs=pl.BlockSpec(memory_space=pltpu.VMEM),
-        scratch_shapes=[pltpu.VMEM((nslot,win,8,LANES),g.dtype),pltpu.VMEM((nslot,win,8,LANES),g.dtype),
-            pltpu.VMEM(((2**ph-1)*ns,win,8,LANES),g.dtype),pltpu.VMEM((2*ns,win,8,LANES),g.dtype),
-            pltpu.SemaphoreType.DMA((nslot,)),pltpu.SemaphoreType.DMA((nsend,)),
-            pltpu.SemaphoreType.DMA((nslot,)),pltpu.SemaphoreType.DMA((nslot,)),
-            pltpu.SemaphoreType.DMA(((2**ph-1)*ns,)),pltpu.SemaphoreType.DMA((2*ns,))],
-        compiler_params=pltpu.CompilerParams(collective_id=1,has_side_effects=True,vmem_limit_bytes=48*1024*1024),
+        scratch_shapes=[pltpu.VMEM((nslot, win, 8, LANES), g.dtype), pltpu.VMEM((nslot, win, 8, LANES), g.dtype)]
+        + buffers + [pltpu.SemaphoreType.DMA((count,)) for count in counts],
+        compiler_params=pltpu.CompilerParams(
+            collective_id=1, has_side_effects=True, vmem_limit_bytes=48 * 1024 * 1024
+        ),
         name="scatter_grads",
     )(g)
 
@@ -1035,7 +1150,7 @@
     scores = lax.dot_general(q, k, (((1,), (1,)), ((), ())), preferred_element_type=jnp.float32)
     spread = jnp.broadcast_to(line, (block, width))
     bias = pltpu.roll(spread, width - block + 1, 1, stride=1, stride_axis=0)[:, :full]
-    return jnp.where(valid, scores * (1.0 / math.sqrt(HD)) + bias, -jnp.inf)
+    return jnp.where(valid, scores + bias, -jnp.inf)
 
 
 def remote(source, target, send, recv, device):
@@ -1110,7 +1225,8 @@
             pl.when(team.main)(relays[i].start)
         part = all_out[b]
         at = pl.ds(pl.multiple_of(b * block, block), block)
-        q_out[at, :] = (forward_dot(part, w_q[...]) + bias_q).astype(jnp.bfloat16)
+        query = (forward_dot(part, w_q[...]) + bias_q).astype(jnp.bfloat16).astype(jnp.float32)
+        q_out[at, :] = (query * (1.0 / math.sqrt(HD))).astype(jnp.bfloat16)
         k_out[at, :] = forward_dot(part, w_k[...]).astype(jnp.bfloat16)
         v_out[at, :] = (forward_dot(part, w_v[...]) + bias_v).astype(jnp.bfloat16)
     full = count * block
@@ -1126,19 +1242,24 @@
     def _(i):
         b = lax.rem(z + 1 + i, count)
         at = pl.ds(pl.multiple_of(b * block, block), block)
-        lse = jnp.zeros((block, 128), jnp.float32)
-        for h in range(H // 2):
-            cols = slice(h * HD, (h + 1) * HD)
-            line = tables[b, pl.ds(c * (H // 2) + h, 1), :]
-            scores = head_scores(q_out[at, cols], k_out[:, cols], line, valid)
-            top = jnp.max(scores, -1, keepdims=True)
-            weights = jnp.exp(scores - top)
-            total = jnp.sum(weights, -1, keepdims=True)
-            probs = (weights * (1.0 / total)).astype(jnp.bfloat16)
-            ctx = jnp.dot(probs, v_out[:, cols], preferred_element_type=jnp.float32)
-            held[b, :, cols] = ctx.astype(jnp.bfloat16)
-            lse = jnp.where(lane == h, top + jnp.log(total), lse)
-        lse_out[at, :] = lse
+        lse_out[at, :] = jnp.zeros((block, 128), jnp.float32)
+
+        @pl.loop(0, H // 4)
+        def _(pair):
+            lanes = pl.ds(pl.multiple_of(pair * 128, 128), 128)
+            both = []
+            for part in range(2):
+                h, cols = 2 * pair + part, slice(part * HD, (part + 1) * HD)
+                line = tables[b, pl.ds(c * (H // 2) + h, 1), :]
+                scores = head_scores(q_out[at, lanes][:, cols], k_out[:, lanes][:, cols], line, valid)
+                top = jnp.max(scores, -1, keepdims=True)
+                weights = jnp.exp(scores - top)
+                total = jnp.sum(weights, -1, keepdims=True)
+                probs = (weights * (1.0 / total)).astype(jnp.bfloat16)
+                both.append(jnp.dot(probs, v_out[:, lanes][:, cols], preferred_element_type=jnp.float32))
+                lse_out[at, :] = jnp.where(lane == h, top + jnp.log(total), lse_out[at, :])
+            held[b, :, lanes] = jnp.concatenate(both, 1).astype(jnp.bfloat16)
+
         own = jnp.logical_and(b == z, team.main)
 
         @pl.when(own)
@@ -1202,6 +1323,7 @@
     valid = lax.broadcasted_iota(jnp.int32, (1, full), 1) < length[pl.ds(team.slot, 1), :][:, 0:1]
     rows = (((0,), (0,)), ((), ()))
     inv = 1.0 / math.sqrt(HD)
+    lane = lax.broadcasted_iota(jnp.int32, (block, 128), 1)
 
     @pl.loop(0, count)
     def _(i):
@@ -1210,38 +1332,47 @@
         copy = remote(d_in.at[b], d_in.at[b], in_send.at[0], in_recv.at[b], (team.di, z))
         pl.when(jnp.logical_not(own))(copy.wait_recv)
         at = pl.ds(pl.multiple_of(b * block, block), block)
-        totals = []
-        for h in range(H // 2):
-            cols = slice(h * HD, (h + 1) * HD)
-            q, k, v = q_all[at, cols], k_all[:, cols], v_all[:, cols]
-            dctx = d_in[b, :, cols]
-            line = tables[b, pl.ds(c * (H // 2) + h, 1), :]
-            width = line.shape[1]
-            scores = head_scores(q, k, line, valid)
-            probs = jnp.exp(scores - lse_all[at, h : h + 1])
-            d_probs = lax.dot_general(dctx, v, (((1,), (1,)), ((), ())), preferred_element_type=jnp.float32)
-            delta = jnp.sum(probs * d_probs, -1, keepdims=True)
-            d_scores = probs * (d_probs - delta)
-            d_scores_b = d_scores.astype(jnp.bfloat16)
-            dq = jnp.dot(d_scores_b, k, preferred_element_type=jnp.float32) * inv
-            totals.append(total_rows(dq))
-            dk_sum[:, cols] += lax.dot_general(d_scores_b, q, rows, preferred_element_type=jnp.float32)
-            dv_sum[:, cols] += lax.dot_general(
-                probs.astype(jnp.bfloat16), dctx, rows, preferred_element_type=jnp.float32
-            )
-            dq_part[at, cols] = dq.astype(jnp.bfloat16)
-            wide = jnp.concatenate([d_scores, jnp.zeros((block, width - full), jnp.float32)], 1)
-            folded = pltpu.roll(wide[0:8], block - 1, 1)
-            for g in range(1, block // 8):
-                folded = folded + pltpu.roll(wide[8 * g : 8 * g + 8], block - 1 - 8 * g, 1)
-            line = folded[0:1]
-            for r in range(1, 8):
-                line = line + pltpu.roll(folded[r : r + 1], width - r, 1)
-            dt_out[b, pl.ds(c * (H // 2) + h, 1), :] = line
-        vec_out[0:1, team.half] += jnp.concatenate(totals, 1)
+
+        @pl.loop(0, H // 4)
+        def _(pair):
+            lanes = pl.ds(pl.multiple_of(pair * 128, 128), 128)
+            parts = []
+            for part in range(2):
+                h, cols = 2 * pair + part, slice(part * HD, (part + 1) * HD)
+                q, k, v = q_all[at, lanes][:, cols], k_all[:, lanes][:, cols], v_all[:, lanes][:, cols]
+                dctx = d_in[b, :, lanes][:, cols]
+                line = tables[b, pl.ds(c * (H // 2) + h, 1), :]
+                width = line.shape[1]
+                lse = jnp.sum(jnp.where(lane == h, lse_all[at, :], 0.0), -1, keepdims=True)
+                probs = jnp.exp(head_scores(q, k, line, valid) - lse)
+                d_probs = lax.dot_general(
+                    dctx, v, (((1,), (1,)), ((), ())), preferred_element_type=jnp.float32
+                )
+                delta = jnp.sum(probs * d_probs, -1, keepdims=True)
+                d_scores = probs * (d_probs - delta)
+                d_scores_b = d_scores.astype(jnp.bfloat16)
+                parts.append((
+                    jnp.dot(d_scores_b, k, preferred_element_type=jnp.float32) * inv,
+                    lax.dot_general(d_scores_b, q, rows, preferred_element_type=jnp.float32),
+                    lax.dot_general(probs.astype(jnp.bfloat16), dctx, rows, preferred_element_type=jnp.float32),
+                ))
+                wide = jnp.concatenate([d_scores, jnp.zeros((block, width - full), jnp.float32)], 1)
+                folded = pltpu.roll(wide[0:8], block - 1, 1)
+                for g in range(1, block // 8):
+                    folded = folded + pltpu.roll(wide[8 * g : 8 * g + 8], block - 1 - 8 * g, 1)
+                line = folded[0:1]
+                for r in range(1, 8):
+                    line = line + pltpu.roll(folded[r : r + 1], width - r, 1)
+                dt_out[b, pl.ds(c * (H // 2) + h, 1), :] = line
+            dq, dk, dv = [jnp.concatenate(values, 1) for values in zip(*parts)]
+            dq_part[at, lanes] = dq.astype(jnp.bfloat16)
+            dk_sum[:, lanes] += dk
+            dv_sum[:, lanes] += dv
+            mine = pl.ds(pl.multiple_of(c * (D // 2) + pair * 128, 128), 128)
+            vec_out[0:1, mine] += total_rows(dq)
 
     vec_out[1:2, team.half] = total_rows(dv_sum[...])
-    dk_part = (dk_sum[...] * inv).astype(jnp.bfloat16)
+    dk_part = dk_sum[...].astype(jnp.bfloat16)
     dk_out[:, team.half] = dk_part
     dv_part = dv_sum[...].astype(jnp.bfloat16)
     dv_out[:, team.half] = dv_part

time: 298 us -> 287 us (0.963)
  Pallas kernels: 278 us -> 266 us
    pallas_call x1, Pallas kernels: 68.3 us -> 61.6 us  [scatter(): pl.pallas_call(functools.partial(scatter_kernel, plan), out_shape=jax.Sha...]
    pallas_call x1, Pallas kernels: 62.5 us -> 57.2 us  [gather(): pl.pallas_call(functools.partial(gather_kernel, plan), out_shape=jax.Shap...]
where the time goes in v2:
time: 287 us; the launch traced here: 286 us
  Pallas kernels  266 us (93%)
  local copies, waits for them, and re-layouts  9.92 us (3%)
  between operations  4.01 us (1%)
  other arithmetic  3.41 us (1%)
    pallas_call x2, Pallas kernels, stage(): pl.pallas_call(lambda *refs: kernel(plan, types.SimpleNamespace(**dict(zi...  128 us
    pallas_call x1, Pallas kernels, scatter(): pl.pallas_call(functools.partial(scatter_kernel, plan), out_shape=jax.Sha...  61.6 us
    pallas_call x1, Pallas kernels, gather(): pl.pallas_call(functools.partial(gather_kernel, plan), out_shape=jax.Shap...  57.2 us
    pallas_call x1, Pallas kernels, weight_grads(): pl.pallas_call(functools.partial(weight_kernel, plan, names, places), out...  19.6 us

profile of v2, /device:TPU:9, one launch (start us, length us, event | category | flops | bytes accessed | tf_op | source)
XLA Modules:
  0.0 285.5 jit_solution(6779094786808100212)
XLA Ops:
  0.6 0.9 pad_slice_fusion
  1.6 0.0 copy-start.5
  1.6 2.0 pad_bitcast_fusion.x
  3.6 57.2 %gather_params.1 = bf16[1486,8,512]{2,1,0:T(8,128)(2,1)} custom-call(f32[1480,128]{1,0:T(8,128)} %pad_bitcast_fusion.x), custom_call_target="tpu_custom_call" | custom-call | tf_op jit(solution)/shard_map/gather_params/pallas_call | solution.py:417
  60.8 0.7 slice_reduce_fusion
  61.5 0.1 reshape.90
  61.6 0.9 convolution_bitcast_fusion.refs_3_
  62.5 0.1 compare_convert_fusion
  62.6 0.9 reshape.100.refs_1_
  63.4 0.7 broadcast_in_dim.2.refs_2_
  64.1 55.5 %forward.1 = (f32[384,512]{1,0:T(8,128)}, bf16[4,512,512]{2,1,0:T(8,128)(2,1)}, bf16[2,192,512]{2,1,0:T(8,128)(2,1)}, bf16[4,192,512]{2,1,0:T(8,128)(2,1)}, bf16...) custom-call(f32[384,512]{1,0:T(8,128)} %bitcast.34, ...), custom_call_target="tpu_custom_call" | custom-call | tf_op jit(solution)/shard_map/forward/pallas_call | solution.py:1471
  119.6 72.2 %backward.1 = (f32[384,512]{1,0:T(8,128)}, f32[384,512]{1,0:T(8,128)}, bf16[384,512]{1,0:T(8,128)(2,1)}, bf16[384,512]{1,0:T(8,128)(2,1)}, bf16[384,2048]{1,0:T(...) custom-call(f32[384,512]{1,0:T(8,128)} %bitcast.35, ...), custom_call_target="tpu_custom_call" | custom-call | tf_op jit(solution)/shard_map/backward/pallas_call | solution.py:1471
  191.8 1.3 convolution_bitcast_fusion.1
  193.1 0.7 reshape.95.refs_25_
  193.8 19.6 %weight_grads.1.g = bf16[1487,8,512]{2,1,0:T(8,128)(2,1)} custom-call(bf16[768,512]{1,0:T(8,128)(2,1)} %bitcast.30, bf16[768,512]{1,0:T(8,128)(2,1)} %get-tuple-element.61.refs_1_, bf16[768,512]{1,0:T(8,128)(2,1)} %bitcast.31, bf16[768,512]{1,0:T(8,128)(2,1)} %get-tuple-element.62.refs_3_, bf16[768,512]{1,0:T(8,128)(2,1)} %bitcast.32, ...), custom_call_target="tpu_custom_call" | custom-call | tf_op jit(solution)/shard_map/weight_grads/pallas_call | solution.py:677
  213.4 0.0 copy-start.4
  213.4 61.6 %scatter_grads.1 = f32[48,8,512]{2,1,0:T(8,128)S(1)} custom-call(bf16[1487,8,512]{2,1,0:T(8,128)(2,1)} %weight_grads.1.g), custom_call_target="tpu_custom_call" | custom-call | tf_op jit(solution)/shard_map/scatter_grads/pallas_call | solution.py:601
  275.0 0.2 copy.24
  275.2 0.8 constant_dynamic-slice_fusion
  276.0 0.6 fusion.5
  279.9 3.3 %multiply_subtract_fusion = (f32[189368]{0:T(1024)}, f32[189368]{0:T(1024)}, f32[189368]{0:T(1024)}, f32[189368]{0:T(1024)}) fusion(f32[189368]{0:T(1024)S(1)} %copy-done, f32[189368]{0:T(1024)S(1)} %copy-done.3, f32[189368]{0:T(1024)S(1)} %copy-done.4, f32[196608]{0:T(1024)S(1)} %bitcast.33, s32[]{:T(128)S(6)} %select_n.15, s32[]{:T(128)S(6)} %select_n.14, ...), kind=kLoop, calls=%fused_computation.4 | loop fusion | flops 3219256 | bytes 6817260 | tf_op jit(solution)/shard_map/sub | solution.py:704
  283.2 0.9 copy.27
  284.1 0.5 copy-done.1
  284.6 0.9 copy.28
  (14 shorter events, 0.1 us)
Async XLA Ops:
  1.6 60.0 %copy-start.5 = (s32[4,1024]{1,0:T(4,128)}, s32[4,1024]{1,0:T(4,128)S(1)}, u32[]{:S(2)}) copy-start(s32[4,1024]{1,0:T(4,128)S(1)} %pad_add_fusion) | copy-start | bytes 49156
  3.6 58.8 %copy-start.6 = (s32[2]{0:T(128)S(1)}, s32[2]{0:T(128)}, u32[]{:S(2)}) copy-start(s32[2]{0:T(128)} %param.9) | copy-start | bytes 28
  213.4 66.5 %copy-start.4 = (f32[189368]{0:T(1024)S(1)}, f32[189368]{0:T(1024)}, u32[]{:S(2)}) copy-start(f32[189368]{0:T(1024)} %param.13) | copy-start | bytes 2272420
  275.0 4.9 %copy-start = (f32[189368]{0:T(1024)S(1)}, f32[189368]{0:T(1024)}, u32[]{:S(2)}) copy-start(f32[189368]{0:T(1024)} %param.11) | copy-start | bytes 2272420
  275.0 4.9 %copy-start.3 = (f32[189368]{0:T(1024)S(1)}, f32[189368]{0:T(1024)}, u32[]{:S(2)}) copy-start(f32[189368]{0:T(1024)} %param.12) | copy-start | bytes 2272420
  279.9 3.3 %copy-start.2 = (f32[384,512]{1,0:T(8,128)S(1)}, f32[384,512]{1,0:T(8,128)}, u32[]{:S(2)}) copy-start(f32[384,512]{1,0:T(8,128)} %get-tuple-element.58) | copy-start | bytes 2359300
  283.2 1.4 copy-start.1
